TPU v7x, 512 devices: a whole 4x8x8 slice. The times are simulated.
512 devices in a mesh: batch: 8 (over y_lo, x), rows: 8 (over z), chan: 8 (over y_hi, core).
Axes of the slice: x: 4, y: 8 (y_hi: 4, y_lo: 2; y = y_hi * 2 + y_lo), z: 8, core: 2. Of those that a mesh axis runs over, the one named last changes fastest.
Arguments:
- images: float32 [64, 24, 64, 32], P('batch', None, ('rows', 'chan')), may hold values from -6 to 6
- shift_mid: float32 [3, 24], replicated, may hold values from -1.75 to 1.75
- gain_mid: float32 [3, 24], replicated, may hold values from -0.3 to 0.3
- lower_mid: float32 [3, 24, 24], replicated, may hold values from -1.25 to 1.25
- upper_mid: float32 [3, 24, 24], replicated, may hold values from -1.25 to 1.25
- diag_mid: float32 [3, 24], replicated, may hold values from -0.3 to 0.3
- first_mid: bfloat16 [3, 9, 12, 512], replicated, may hold values from -0.625 to 0.625
- first_bias_mid: bfloat16 [3, 512], replicated, may hold values from -3 to 3
- second_mid: bfloat16 [3, 512, 512], replicated, may hold values from -0.25 to 0.25
- second_bias_mid: float32 [3, 512], replicated, may hold values from -3 to 3
- third_mid: bfloat16 [3, 9, 512, 24], replicated, may hold values from -0.09375 to 0.09375
- third_bias_mid: float32 [3, 24], replicated, may hold values from -3 to 3
- shift_top: float32 [2, 48], replicated, may hold values from -1.75 to 1.75
- gain_top: float32 [2, 48], replicated, may hold values from -0.3 to 0.3
- lower_top: float32 [2, 48, 48], replicated, may hold values from -0.875 to 0.875
- upper_top: float32 [2, 48, 48], replicated, may hold values from -0.875 to 0.875
- diag_top: float32 [2, 48], replicated, may hold values from -0.3 to 0.3
- first_top: bfloat16 [2, 9, 24, 512], replicated, may hold values from -0.4375 to 0.4375
- first_bias_top: bfloat16 [2, 512], replicated, may hold values from -3 to 3
- second_top: bfloat16 [2, 512, 512], replicated, may hold values from -0.25 to 0.25
- second_bias_top: float32 [2, 512], replicated, may hold values from -3 to 3
- third_top: bfloat16 [2, 9, 512, 48], replicated, may hold values from -0.09375 to 0.09375
- third_bias_top: float32 [2, 48], replicated, may hold values from -3 to 3
Outputs:
- latent_mid: float32 [64, 12, 64, 32], P('batch', None, ('rows', 'chan'))
- latent_top: float32 [64, 48, 32, 16], P(('batch', 'chan'), None, 'rows')
- loglik: float32 [64], P(('batch', 'chan'))
All inputs are finite; a program needn't handle non-finite values.
Results may differ from a plain program's by a relative error of at most 0.008.
Values may be sent and summed in bfloat16 or wider, within the bound.
A program may use at most 64 MiB of HBM per device.

v0:
```python
import math

import jax
import jax.numpy as jnp
from jax import lax
from jax.sharding import PartitionSpec as P

log_two_pi = math.log(2.0 * math.pi)


def padded_2(x, sides, width):
    edges = {}
    for axis, dim in sides:
        size, length = (lax.axis_size(axis), x.shape[dim])
        up = [(i, (i + 1) % size) for i in range(size - 1)]
        last = lax.slice_in_dim(x, length - width, length, axis=dim)
        first = lax.slice_in_dim(x, 0, width, axis=dim)
        edges[dim] = (
            lax.ppermute(last, axis, up),
            lax.ppermute(first, axis, [(b, a) for a, b in up]),
        )
    done = []
    for _, dim in sides:
        low, high = edges[dim]
        around = [(width, width) if d in done else (0, 0) for d in range(x.ndim)]
        x = jnp.concatenate([jnp.pad(low, around), x, jnp.pad(high, around)], axis=dim)
        done.append(dim)
    return x


def with_halo(block, sides, width):
    for axis, dim in sides:
        count = lax.axis_size(axis)
        forward = [(i, i + 1) for i in range(count - 1)]
        backward = [(target, source) for source, target in forward]
        low = lax.ppermute(
            lax.slice_in_dim(block, block.shape[dim] - width, None, axis=dim), axis, forward
        )
        high = lax.ppermute(lax.slice_in_dim(block, 0, width, axis=dim), axis, backward)
        block = jnp.concatenate([low, block, high], axis=dim)
    return block


def in_blocks(x, dim, length):
    lengths = x.shape
    pieces = x.reshape(*lengths[:dim], length, lengths[dim] // length, *lengths[dim + 1 :])
    return jnp.moveaxis(pieces, dim, 0)


def summed_on_arrival(x, axis, dim):
    length = lax.axis_size(axis)
    pieces = lax.all_to_all(in_blocks(x, dim, length), axis, 0, 0, tiled=True)
    return jnp.sum(pieces, axis=0)


def sent_to_all(x, axis):
    copies = jnp.broadcast_to(x, (lax.axis_size(axis), *x.shape))
    return lax.all_to_all(copies, axis, split_axis=0, concat_axis=0, tiled=True)


def over_copies(x, axis):
    everything = sent_to_all(x, axis)
    return jnp.sum(everything, axis=0)


def conv_in(rimmed, weights, rows_out):
    columns = rimmed.shape[3]
    padded = jnp.pad(rimmed, ((0, 0), (0, 0), (0, 0), (1, 1)))
    summed = None
    for tap_idx in range(9):
        row_off = tap_idx // 3
        col_off = tap_idx % 3
        window = padded[:, :, row_off : row_off + rows_out, col_off : col_off + columns]
        contrib = jnp.einsum(
            "bchw,co->bhwo", window, weights[tap_idx], preferred_element_type=jnp.float32
        )
        summed = contrib if summed is None else summed + contrib
    return summed


def conv_out(rimmed, weights):
    rows_out = rimmed.shape[1] - 2
    columns = rimmed.shape[2]
    padded = jnp.pad(rimmed, ((0, 0), (0, 0), (1, 1), (0, 0)))
    summed = None
    for tap_idx in range(9):
        row_off = tap_idx // 3
        col_off = tap_idx % 3
        window = padded[:, row_off : row_off + rows_out, col_off : col_off + columns, :]
        contrib = jnp.einsum(
            "bhwc,co->bohw", window, weights[tap_idx], preferred_element_type=jnp.float32
        )
        summed = contrib if summed is None else summed + contrib
    return summed


def hidden_layers(widened, first_w, first_b, second_w, second_b, rows_out):
    inner = conv_in(widened, first_w, rows_out) + first_b.astype(jnp.float32)[None, None, None, :]
    inner = jax.nn.relu(inner).astype(jnp.bfloat16)
    middle = jnp.einsum("bhwc,co->bhwo", inner, second_w, preferred_element_type=jnp.float32)
    return jax.nn.relu(middle + second_b[None, None, None, :])


def mid_hidden(coupled, first_w, first_b, second_w, second_b):
    rimmed = padded_2(coupled, ((("rows", "chan"), 2),), 1)
    middle = hidden_layers(rimmed, first_w, first_b, second_w, second_b, coupled.shape[2]).astype(
        jnp.bfloat16
    )
    return padded_2(middle, ((("rows", "chan"), 1),), 1)


def top_hidden(coupled, first_w, first_b, second_w, second_b):
    rimmed = with_halo(coupled, (("rows", 2),), 1)
    middle = hidden_layers(rimmed, first_w, first_b, second_w, second_b, coupled.shape[2]).astype(
        jnp.bfloat16
    )
    return with_halo(middle, (("rows", 1),), 1)


def flow_step(flow_state, params, hidden_fn):
    (
        shift_vec,
        gain_vec,
        lower_raw,
        upper_raw,
        diag_log,
        first_w,
        first_b,
        second_w,
        second_b,
        third_w,
        third_b,
    ) = params
    channels = flow_state.shape[1]
    half_chan = channels // 2
    cell_count = flow_state.shape[2] * flow_state.shape[3]
    mixed_state = (flow_state + shift_vec[None, :, None, None]) * jnp.exp(gain_vec)[
        None, :, None, None
    ]
    lower_mat = jnp.tril(lower_raw, -1) + jnp.eye(channels, dtype=jnp.float32)
    upper_mat = jnp.triu(upper_raw, 1) + jnp.diag(jnp.exp(diag_log))
    matrix = jnp.dot(lower_mat, upper_mat, precision=lax.Precision.HIGHEST)
    mixed_state = jnp.einsum("oc,bchw->bohw", matrix, mixed_state, precision=lax.Precision.HIGHEST)
    part_a = mixed_state[:, :half_chan]
    part_b = mixed_state[:, half_chan:]
    coupled = part_a.astype(jnp.bfloat16)
    rim_middle = hidden_fn(coupled, first_w, first_b, second_w, second_b)
    output = conv_out(rim_middle, third_w) + third_b[None, :, None, None]
    gate_pre = output[:, :half_chan] + 2.0
    updated = (part_b + output[:, half_chan:]) * jax.nn.sigmoid(gate_pre)
    step_term = cell_count * (jnp.sum(gain_vec) + jnp.sum(diag_log)) + jnp.sum(
        jax.nn.log_sigmoid(gate_pre), axis=(1, 2, 3)
    )
    return (jnp.concatenate([part_a, updated], axis=1), step_term)


def scale_pass(flow_state, params, hidden_fn):
    logdet = jnp.zeros((flow_state.shape[0],), jnp.float32)
    for step_num in range(params[0].shape[0]):
        flow_state, step_term = flow_step(
            flow_state, tuple((p[step_num] for p in params)), hidden_fn
        )
        logdet = logdet + step_term
    return (flow_state, logdet)


def gauss_terms(latent):
    return -0.5 * jnp.sum(latent * latent, axis=(1, 2, 3)) - 0.5 * log_two_pi * latent[0].size


def body(
    images,
    shift_mid,
    gain_mid,
    lower_mid,
    upper_mid,
    diag_mid,
    first_mid,
    first_bias_mid,
    second_mid,
    second_bias_mid,
    third_mid,
    third_bias_mid,
    shift_top,
    gain_top,
    lower_top,
    upper_top,
    diag_top,
    first_top,
    first_bias_top,
    second_top,
    second_bias_top,
    third_top,
    third_bias_top,
):
    params_mid = (
        shift_mid,
        gain_mid,
        lower_mid,
        upper_mid,
        diag_mid,
        first_mid,
        first_bias_mid,
        second_mid,
        second_bias_mid,
        third_mid,
        third_bias_mid,
    )
    params_top = (
        shift_top,
        gain_top,
        lower_top,
        upper_top,
        diag_top,
        first_top,
        first_bias_top,
        second_top,
        second_bias_top,
        third_top,
        third_bias_top,
    )
    images_dev, channels, height, columns = images.shape
    flow_state, logdet_mid = scale_pass(images, params_mid, mid_hidden)
    half_chan = channels // 2
    latent_mid = flow_state[:, :half_chan]
    kept_chan = flow_state[:, half_chan:]
    mid_part = gauss_terms(latent_mid) + logdet_mid
    grouped = lax.all_to_all(kept_chan, "chan", split_axis=0, concat_axis=2, tiled=True)
    group_imgs, group_chan, group_rows, group_cols = grouped.shape
    squeezed = grouped.reshape(
        group_imgs, group_chan, group_rows // 2, 2, group_cols // 2, 2
    ).transpose(0, 1, 3, 5, 2, 4)
    squeezed = squeezed.reshape(group_imgs, group_chan * 4, group_rows // 2, group_cols // 2)
    latent_top, logdet_top = scale_pass(squeezed, params_top, top_hidden)
    top_part = gauss_terms(latent_top) + logdet_top
    mid_own = summed_on_arrival(mid_part, "chan", 0)
    summed = over_copies(mid_own + top_part, "rows")
    total_dims = channels * height * lax.axis_size("rows") * lax.axis_size("chan") * columns
    return (latent_mid, latent_top, summed / total_dims)


def solution(mesh):
    placed = (
        P("batch", None, ("rows", "chan"), None),
        P(),
        P(),
        P(),
        P(),
        P(),
        P(),
        P(),
        P(),
        P(),
        P(),
        P(),
        P(),
        P(),
        P(),
        P(),
        P(),
        P(),
        P(),
        P(),
        P(),
        P(),
        P(),
    )
    return jax.shard_map(
        body,
        mesh=mesh,
        in_specs=placed,
        out_specs=(
            P("batch", None, ("rows", "chan"), None),
            P(("batch", "chan"), None, "rows", None),
            P(("batch", "chan")),
        ),
        check_vma=False,
    )
```

profile of v0, /device:TPU:1, one launch (start us, length us, event | category | flops | bytes accessed | tf_op | source)
XLA Modules:
  0.0 222.2 jit_solution(14348905123432826290)
XLA Ops:
  5.2 5.6 %collective-permute-start = (bf16[8,12,1,32]{3,1,0,2:T(8,128)(2,1)S(1)}, bf16[8,12,1,32]{3,1,0,2:T(8,128)(2,1)S(1)}, u32[]{:S(2)}, u32[]{:S(2)}) collective-permute-start(bf16[8,12,1,32]{3,1,0,2:T(8,128)(2,1)S(1)} %slice.1913), channel_id=1, source_target_pairs={{0,1},{1,2},{2,3},{3,4},{4,5},{5,6},{6,7},{7,8},{8,9},{9,10},{10,1... | collective-permute-start | bytes 18440 | tf_op jit(solution)/shard_map/ppermute | solution.py:19
  10.8 4.4 %collective-permute-start.1 = (bf16[8,12,1,32]{3,1,0,2:T(8,128)(2,1)S(1)}, bf16[8,12,1,32]{3,1,0,2:T(8,128)(2,1)S(1)}, u32[]{:S(2)}, u32[]{:S(2)}) collective-permute-start(bf16[8,12,1,32]{3,1,0,2:T(8,128)(2,1)S(1)} %slice.1913), channel_id=1, source_target_pairs={{1,0},{2,1},{3,2},{4,3},{5,4},{6,5},{7,6},{8,7},{9,8},{10,9},{11,1... | collective-permute-start | bytes 18440 | tf_op jit(solution)/shard_map/ppermute | solution.py:20
  21.8 2.3 %collective-permute-start.2 = (bf16[8,1,32,512]{3,2,0,1:T(8,128)(2,1)S(1)}, bf16[8,1,32,512]{3,2,0,1:T(8,128)(2,1)S(1)}, u32[]{:S(2)}, u32[]{:S(2)}) collective-permute-start(bf16[8,1,32,512]{3,2,0,1:T(8,128)(2,1)S(1)} %bitcast.923), channel_id=1, source_target_pairs={{0,1},{1,2},{2,3},{3,4},{4,5},{5,6},{6,7},{7,8},{8,9},{9,10},{10,1... | collective-permute-start | bytes 786440 | tf_op jit(solution)/shard_map/ppermute | solution.py:19
  24.1 2.0 collective-permute-start.3
  27.4 10.4 %collective-permute-done.3 = bf16[8,1,32,512]{3,2,0,1:T(8,128)(2,1)S(1)} collective-permute-done((bf16[8,1,32,512]{3,2,0,1:T(8,128)(2,1)S(1)}, bf16[8,1,32,512]{3,2,0,1:T(8,128)(2,1)S(1)}, u32[]{:S(2)}, u32[]{:S(2)}) %collective-permute-start.3) | collective-permute-done | bytes 262176 | tf_op jit(solution)/shard_map/ppermute | solution.py:20
  50.0 2.4 %collective-permute-start.5 = (bf16[8,12,1,32]{3,1,0,2:T(8,128)(2,1)S(1)}, bf16[8,12,1,32]{3,1,0,2:T(8,128)(2,1)S(1)}, u32[]{:S(2)}, u32[]{:S(2)}) collective-permute-start(bf16[8,12,1,32]{3,1,0,2:T(8,128)(2,1)S(1)} %slice.1912), channel_id=1, source_target_pairs={{1,0},{2,1},{3,2},{4,3},{5,4},{6,5},{7,6},{8,7},{9,8},{10,9},{11,1... | collective-permute-start | bytes 18440 | tf_op jit(solution)/shard_map/ppermute | solution.py:20
  52.4 4.9 %collective-permute-done.5 = bf16[8,12,1,32]{3,1,0,2:T(8,128)(2,1)S(1)} collective-permute-done((bf16[8,12,1,32]{3,1,0,2:T(8,128)(2,1)S(1)}, bf16[8,12,1,32]{3,1,0,2:T(8,128)(2,1)S(1)}, u32[]{:S(2)}, u32[]{:S(2)}) %collective-permute-start.5) | collective-permute-done | bytes 6176 | tf_op jit(solution)/shard_map/ppermute | solution.py:20
  62.2 2.4 %collective-permute-start.7 = (bf16[8,1,32,512]{3,2,0,1:T(8,128)(2,1)S(1)}, bf16[8,1,32,512]{3,2,0,1:T(8,128)(2,1)S(1)}, u32[]{:S(2)}, u32[]{:S(2)}) collective-permute-start(bf16[8,1,32,512]{3,2,0,1:T(8,128)(2,1)S(1)} %bitcast.927), channel_id=1, source_target_pairs={{1,0},{2,1},{3,2},{4,3},{5,4},{6,5},{7,6},{8,7},{9,8},{10,9},{11,1... | collective-permute-start | bytes 786440 | tf_op jit(solution)/shard_map/ppermute | solution.py:20
  65.6 6.5 %collective-permute-done.7 = bf16[8,1,32,512]{3,2,0,1:T(8,128)(2,1)S(1)} collective-permute-done((bf16[8,1,32,512]{3,2,0,1:T(8,128)(2,1)S(1)}, bf16[8,1,32,512]{3,2,0,1:T(8,128)(2,1)S(1)}, u32[]{:S(2)}, u32[]{:S(2)}) %collective-permute-start.7) | collective-permute-done | bytes 262176 | tf_op jit(solution)/shard_map/ppermute | solution.py:20
  84.2 2.4 %collective-permute-start.9 = (bf16[8,12,1,32]{3,1,0,2:T(8,128)(2,1)S(1)}, bf16[8,12,1,32]{3,1,0,2:T(8,128)(2,1)S(1)}, u32[]{:S(2)}, u32[]{:S(2)}) collective-permute-start(bf16[8,12,1,32]{3,1,0,2:T(8,128)(2,1)S(1)} %slice.1916), channel_id=1, source_target_pairs={{1,0},{2,1},{3,2},{4,3},{5,4},{6,5},{7,6},{8,7},{9,8},{10,9},{11,1... | collective-permute-start | bytes 18440 | tf_op jit(solution)/shard_map/ppermute | solution.py:20
  87.4 4.5 %collective-permute-done.9 = bf16[8,12,1,32]{3,1,0,2:T(8,128)(2,1)S(1)} collective-permute-done((bf16[8,12,1,32]{3,1,0,2:T(8,128)(2,1)S(1)}, bf16[8,12,1,32]{3,1,0,2:T(8,128)(2,1)S(1)}, u32[]{:S(2)}, u32[]{:S(2)}) %collective-permute-start.9) | collective-permute-done | bytes 6176 | tf_op jit(solution)/shard_map/ppermute | solution.py:20
  96.7 2.4 %collective-permute-start.11 = (bf16[8,1,32,512]{3,2,0,1:T(8,128)(2,1)S(1)}, bf16[8,1,32,512]{3,2,0,1:T(8,128)(2,1)S(1)}, u32[]{:S(2)}, u32[]{:S(2)}) collective-permute-start(bf16[8,1,32,512]{3,2,0,1:T(8,128)(2,1)S(1)} %bitcast.930), channel_id=1, source_target_pairs={{1,0},{2,1},{3,2},{4,3},{5,4},{6,5},{7,6},{8,7},{9,8},{10,9},{11,1... | collective-permute-start | bytes 786440 | tf_op jit(solution)/shard_map/ppermute | solution.py:20
  100.1 8.0 %collective-permute-done.11 = bf16[8,1,32,512]{3,2,0,1:T(8,128)(2,1)S(1)} collective-permute-done((bf16[8,1,32,512]{3,2,0,1:T(8,128)(2,1)S(1)}, bf16[8,1,32,512]{3,2,0,1:T(8,128)(2,1)S(1)}, u32[]{:S(2)}, u32[]{:S(2)}) %collective-permute-start.11) | collective-permute-done | bytes 262176 | tf_op jit(solution)/shard_map/ppermute | solution.py:20
  119.9 7.8 %all-to-all-start = ((f32[8,1,384]{2,1,0:T(1,128)}), f32[8,1,384]{2,1,0:T(1,128)S(1)}, u32[]{:S(2)}, u32[]{:S(2)}) async-start(f32[8,1,384]{2,1,0:T(1,128)} %reshape.1494), calls=%async_computation | async-start | bytes 24576 | tf_op jit(solution)/shard_map/all_to_all | solution.py:228
  128.0 6.8 %all-to-all-done = f32[8,1,384]{2,1,0:T(1,128)S(1)} async-done(((f32[8,1,384]{2,1,0:T(1,128)}), f32[8,1,384]{2,1,0:T(1,128)S(1)}, u32[]{:S(2)}, u32[]{:S(2)}) %all-to-all-start) | async-done | bytes 12320 | tf_op jit(solution)/shard_map/all_to_all | solution.py:228
  136.3 4.0 %collective-permute-start.12 = (bf16[1,24,1,16]{1,3,2,0:T(8,128)(2,1)S(1)}, bf16[1,24,1,16]{1,3,2,0:T(8,128)(2,1)S(1)}, u32[]{:S(2)}, u32[]{:S(2)}) collective-permute-start(bf16[1,24,1,16]{1,3,2,0:T(8,128)(2,1)S(1)} %get-tuple-element.52), channel_id=1, source_target_pairs={{0,8},{8,16},{16,24},{24,32},{32,40},{40,48},{48,56},{1,9},{9,17},... | collective-permute-start | bytes 2312 | tf_op jit(solution)/shard_map/ppermute | solution.py:36
  141.6 3.7 %collective-permute-done.13 = bf16[1,24,1,16]{1,3,2,0:T(8,128)(2,1)S(1)} collective-permute-done((bf16[1,24,1,16]{1,3,2,0:T(8,128)(2,1)S(1)}, bf16[1,24,1,16]{1,3,2,0:T(8,128)(2,1)S(1)}, u32[]{:S(2)}, u32[]{:S(2)}) %collective-permute-start.13) | collective-permute-done | bytes 800 | tf_op jit(solution)/shard_map/ppermute | solution.py:39
  146.9 13.7 %collective-permute-start.14 = (bf16[1,1,16,512]{3,2,1,0:T(8,128)(2,1)S(1)}, bf16[1,1,16,512]{3,2,1,0:T(8,128)(2,1)S(1)}, u32[]{:S(2)}, u32[]{:S(2)}) collective-permute-start(bf16[1,1,16,512]{3,2,1,0:T(8,128)(2,1)S(1)} %get-tuple-element.42), channel_id=1, source_target_pairs={{0,8},{8,16},{16,24},{24,32},{32,40},{40,48},{48,56},{1,9},{9,17},... | collective-permute-start | bytes 49160 | tf_op jit(solution)/shard_map/ppermute | solution.py:36
  167.4 3.4 %collective-permute-start.16 = (bf16[1,24,1,16]{1,3,2,0:T(8,128)(2,1)S(1)}, bf16[1,24,1,16]{1,3,2,0:T(8,128)(2,1)S(1)}, u32[]{:S(2)}, u32[]{:S(2)}) collective-permute-start(bf16[1,24,1,16]{1,3,2,0:T(8,128)(2,1)S(1)} %get-tuple-element.50), channel_id=1, source_target_pairs={{0,8},{8,16},{16,24},{24,32},{32,40},{40,48},{48,56},{1,9},{9,17},... | collective-permute-start | bytes 2312 | tf_op jit(solution)/shard_map/ppermute | solution.py:36
  178.6 4.0 %collective-permute-start.18 = (bf16[1,1,16,512]{3,2,1,0:T(8,128)(2,1)S(1)}, bf16[1,1,16,512]{3,2,1,0:T(8,128)(2,1)S(1)}, u32[]{:S(2)}, u32[]{:S(2)}) collective-permute-start(bf16[1,1,16,512]{3,2,1,0:T(8,128)(2,1)S(1)} %get-tuple-element.40), channel_id=1, source_target_pairs={{0,8},{8,16},{16,24},{24,32},{32,40},{40,48},{48,56},{1,9},{9,17},... | collective-permute-start | bytes 49160 | tf_op jit(solution)/shard_map/ppermute | solution.py:36
  184.6 7.6 %all-to-all-start.1 = ((f32[8,1,1]{2,1,0:T(1,128)}), f32[8,1,1]{2,1,0:T(1,128)S(1)}, u32[]{:S(2)}, u32[]{:S(2)}) async-start(f32[8,1,1]{2,1,0:T(1,128)} %copy.48), calls=%async_computation.1 | async-start | bytes 8192 | tf_op jit(solution)/shard_map/all_to_all | solution.py:52
  192.2 7.0 %all-to-all-done.1 = f32[8,1,1]{2,1,0:T(1,128)S(1)} async-done(((f32[8,1,1]{2,1,0:T(1,128)}), f32[8,1,1]{2,1,0:T(1,128)S(1)}, u32[]{:S(2)}, u32[]{:S(2)}) %all-to-all-start.1) | async-done | bytes 64 | tf_op jit(solution)/shard_map/all_to_all | solution.py:52
  206.4 6.8 %all-to-all-start.2 = ((f32[8,1,1]{2,1,0:T(1,128)}), f32[8,1,1]{2,1,0:T(1,128)S(1)}, u32[]{:S(2)}, u32[]{:S(2)}) async-start(f32[8,1,1]{2,1,0:T(1,128)} %broadcast_in_dim.91), calls=%async_computation.2 | async-start | bytes 8192 | tf_op jit(solution)/shard_map/all_to_all | solution.py:58
  213.9 5.9 %all-to-all-done.2 = f32[8,1,1]{2,1,0:T(1,128)S(1)} async-done(((f32[8,1,1]{2,1,0:T(1,128)}), f32[8,1,1]{2,1,0:T(1,128)S(1)}, u32[]{:S(2)}, u32[]{:S(2)}) %all-to-all-start.2) | async-done | bytes 64 | tf_op jit(solution)/shard_map/all_to_all | solution.py:58
  (203 shorter events, 80.7 us)
Async XLA Ops:
  5.2 11.7 %collective-permute-start = (bf16[8,12,1,32]{3,1,0,2:T(8,128)(2,1)S(1)}, bf16[8,12,1,32]{3,1,0,2:T(8,128)(2,1)S(1)}, u32[]{:S(2)}, u32[]{:S(2)}) collective-permute-start(bf16[8,12,1,32]{3,1,0,2:T(8,128)(2,1)S(1)} %slice.1913), channel_id=1, source_target_pairs={{0,1},{1,2},{2,3},{3,4},{4,5},{5,6},{6,7},{7,8},{8,9},{9,10},{10,1... | collective-permute-start | bytes 18440 | tf_op jit(solution)/shard_map/ppermute | solution.py:19
  10.8 6.1 %collective-permute-start.1 = (bf16[8,12,1,32]{3,1,0,2:T(8,128)(2,1)S(1)}, bf16[8,12,1,32]{3,1,0,2:T(8,128)(2,1)S(1)}, u32[]{:S(2)}, u32[]{:S(2)}) collective-permute-start(bf16[8,12,1,32]{3,1,0,2:T(8,128)(2,1)S(1)} %slice.1913), channel_id=1, source_target_pairs={{1,0},{2,1},{3,2},{4,3},{5,4},{6,5},{7,6},{8,7},{9,8},{10,9},{11,1... | collective-permute-start | bytes 18440 | tf_op jit(solution)/shard_map/ppermute | solution.py:20
  21.8 5.6 %collective-permute-start.2 = (bf16[8,1,32,512]{3,2,0,1:T(8,128)(2,1)S(1)}, bf16[8,1,32,512]{3,2,0,1:T(8,128)(2,1)S(1)}, u32[]{:S(2)}, u32[]{:S(2)}) collective-permute-start(bf16[8,1,32,512]{3,2,0,1:T(8,128)(2,1)S(1)} %bitcast.923), channel_id=1, source_target_pairs={{0,1},{1,2},{2,3},{3,4},{4,5},{5,6},{6,7},{7,8},{8,9},{9,10},{10,1... | collective-permute-start | bytes 786440 | tf_op jit(solution)/shard_map/ppermute | solution.py:19
  24.1 13.7 %collective-permute-start.3 = (bf16[8,1,32,512]{3,2,0,1:T(8,128)(2,1)S(1)}, bf16[8,1,32,512]{3,2,0,1:T(8,128)(2,1)S(1)}, u32[]{:S(2)}, u32[]{:S(2)}) collective-permute-start(bf16[8,1,32,512]{3,2,0,1:T(8,128)(2,1)S(1)} %bitcast.924), channel_id=1, source_target_pairs={{1,0},{2,1},{3,2},{4,3},{5,4},{6,5},{7,6},{8,7},{9,8},{10,9},{11,1... | collective-permute-start | bytes 786440 | tf_op jit(solution)/shard_map/ppermute | solution.py:20
  48.1 4.4 %collective-permute-start.4 = (bf16[8,12,1,32]{3,1,0,2:T(8,128)(2,1)S(1)}, bf16[8,12,1,32]{3,1,0,2:T(8,128)(2,1)S(1)}, u32[]{:S(2)}, u32[]{:S(2)}) collective-permute-start(bf16[8,12,1,32]{3,1,0,2:T(8,128)(2,1)S(1)} %slice.1912), channel_id=1, source_target_pairs={{0,1},{1,2},{2,3},{3,4},{4,5},{5,6},{6,7},{7,8},{8,9},{9,10},{10,1... | collective-permute-start | bytes 18440 | tf_op jit(solution)/shard_map/ppermute | solution.py:19
  50.0 7.3 %collective-permute-start.5 = (bf16[8,12,1,32]{3,1,0,2:T(8,128)(2,1)S(1)}, bf16[8,12,1,32]{3,1,0,2:T(8,128)(2,1)S(1)}, u32[]{:S(2)}, u32[]{:S(2)}) collective-permute-start(bf16[8,12,1,32]{3,1,0,2:T(8,128)(2,1)S(1)} %slice.1912), channel_id=1, source_target_pairs={{1,0},{2,1},{3,2},{4,3},{5,4},{6,5},{7,6},{8,7},{9,8},{10,9},{11,1... | collective-permute-start | bytes 18440 | tf_op jit(solution)/shard_map/ppermute | solution.py:20
  60.2 5.3 %collective-permute-start.6 = (bf16[8,1,32,512]{3,2,0,1:T(8,128)(2,1)S(1)}, bf16[8,1,32,512]{3,2,0,1:T(8,128)(2,1)S(1)}, u32[]{:S(2)}, u32[]{:S(2)}) collective-permute-start(bf16[8,1,32,512]{3,2,0,1:T(8,128)(2,1)S(1)} %bitcast.926), channel_id=1, source_target_pairs={{0,1},{1,2},{2,3},{3,4},{4,5},{5,6},{6,7},{7,8},{8,9},{9,10},{10,1... | collective-permute-start | bytes 786440 | tf_op jit(solution)/shard_map/ppermute | solution.py:19
  62.2 9.9 %collective-permute-start.7 = (bf16[8,1,32,512]{3,2,0,1:T(8,128)(2,1)S(1)}, bf16[8,1,32,512]{3,2,0,1:T(8,128)(2,1)S(1)}, u32[]{:S(2)}, u32[]{:S(2)}) collective-permute-start(bf16[8,1,32,512]{3,2,0,1:T(8,128)(2,1)S(1)} %bitcast.927), channel_id=1, source_target_pairs={{1,0},{2,1},{3,2},{4,3},{5,4},{6,5},{7,6},{8,7},{9,8},{10,9},{11,1... | collective-permute-start | bytes 786440 | tf_op jit(solution)/shard_map/ppermute | solution.py:20
  82.3 5.1 %collective-permute-start.8 = (bf16[8,12,1,32]{3,1,0,2:T(8,128)(2,1)S(1)}, bf16[8,12,1,32]{3,1,0,2:T(8,128)(2,1)S(1)}, u32[]{:S(2)}, u32[]{:S(2)}) collective-permute-start(bf16[8,12,1,32]{3,1,0,2:T(8,128)(2,1)S(1)} %slice.1916), channel_id=1, source_target_pairs={{0,1},{1,2},{2,3},{3,4},{4,5},{5,6},{6,7},{7,8},{8,9},{9,10},{10,1... | collective-permute-start | bytes 18440 | tf_op jit(solution)/shard_map/ppermute | solution.py:19
  84.2 7.7 %collective-permute-start.9 = (bf16[8,12,1,32]{3,1,0,2:T(8,128)(2,1)S(1)}, bf16[8,12,1,32]{3,1,0,2:T(8,128)(2,1)S(1)}, u32[]{:S(2)}, u32[]{:S(2)}) collective-permute-start(bf16[8,12,1,32]{3,1,0,2:T(8,128)(2,1)S(1)} %slice.1916), channel_id=1, source_target_pairs={{1,0},{2,1},{3,2},{4,3},{5,4},{6,5},{7,6},{8,7},{9,8},{10,9},{11,1... | collective-permute-start | bytes 18440 | tf_op jit(solution)/shard_map/ppermute | solution.py:20
  94.8 5.3 %collective-permute-start.10 = (bf16[8,1,32,512]{3,2,0,1:T(8,128)(2,1)S(1)}, bf16[8,1,32,512]{3,2,0,1:T(8,128)(2,1)S(1)}, u32[]{:S(2)}, u32[]{:S(2)}) collective-permute-start(bf16[8,1,32,512]{3,2,0,1:T(8,128)(2,1)S(1)} %bitcast.929), channel_id=1, source_target_pairs={{0,1},{1,2},{2,3},{3,4},{4,5},{5,6},{6,7},{7,8},{8,9},{9,10},{10,1... | collective-permute-start | bytes 786440 | tf_op jit(solution)/shard_map/ppermute | solution.py:19
  96.7 11.4 %collective-permute-start.11 = (bf16[8,1,32,512]{3,2,0,1:T(8,128)(2,1)S(1)}, bf16[8,1,32,512]{3,2,0,1:T(8,128)(2,1)S(1)}, u32[]{:S(2)}, u32[]{:S(2)}) collective-permute-start(bf16[8,1,32,512]{3,2,0,1:T(8,128)(2,1)S(1)} %bitcast.930), channel_id=1, source_target_pairs={{1,0},{2,1},{3,2},{4,3},{5,4},{6,5},{7,6},{8,7},{9,8},{10,9},{11,1... | collective-permute-start | bytes 786440 | tf_op jit(solution)/shard_map/ppermute | solution.py:20
  114.8 30.5 %copy-start.3 = (bf16[2,9,24,512]{3,2,1,0:T(8,128)(2,1)S(1)}, bf16[2,9,24,512]{3,2,1,0:T(8,128)(2,1)}, u32[]{:S(2)}) copy-start(bf16[2,9,24,512]{3,2,1,0:T(8,128)(2,1)} %param.40) | copy-start | bytes 1327108
  119.9 14.9 %all-to-all-start = ((f32[8,1,384]{2,1,0:T(1,128)}), f32[8,1,384]{2,1,0:T(1,128)S(1)}, u32[]{:S(2)}, u32[]{:S(2)}) async-start(f32[8,1,384]{2,1,0:T(1,128)} %reshape.1494), calls=%async_computation | async-start | bytes 24576 | tf_op jit(solution)/shard_map/all_to_all | solution.py:228
  136.3 5.3 %collective-permute-start.12 = (bf16[1,24,1,16]{1,3,2,0:T(8,128)(2,1)S(1)}, bf16[1,24,1,16]{1,3,2,0:T(8,128)(2,1)S(1)}, u32[]{:S(2)}, u32[]{:S(2)}) collective-permute-start(bf16[1,24,1,16]{1,3,2,0:T(8,128)(2,1)S(1)} %get-tuple-element.52), channel_id=1, source_target_pairs={{0,8},{8,16},{16,24},{24,32},{32,40},{40,48},{48,56},{1,9},{9,17},... | collective-permute-start | bytes 2312 | tf_op jit(solution)/shard_map/ppermute | solution.py:36
  140.3 5.0 %collective-permute-start.13 = (bf16[1,24,1,16]{1,3,2,0:T(8,128)(2,1)S(1)}, bf16[1,24,1,16]{1,3,2,0:T(8,128)(2,1)S(1)}, u32[]{:S(2)}, u32[]{:S(2)}) collective-permute-start(bf16[1,24,1,16]{1,3,2,0:T(8,128)(2,1)S(1)} %get-tuple-element.53), channel_id=1, source_target_pairs={{8,0},{16,8},{24,16},{32,24},{40,32},{48,40},{56,48},{9,1},{17,9},... | collective-permute-start | bytes 2312 | tf_op jit(solution)/shard_map/ppermute | solution.py:39
  146.9 16.5 %collective-permute-start.14 = (bf16[1,1,16,512]{3,2,1,0:T(8,128)(2,1)S(1)}, bf16[1,1,16,512]{3,2,1,0:T(8,128)(2,1)S(1)}, u32[]{:S(2)}, u32[]{:S(2)}) collective-permute-start(bf16[1,1,16,512]{3,2,1,0:T(8,128)(2,1)S(1)} %get-tuple-element.42), channel_id=1, source_target_pairs={{0,8},{8,16},{16,24},{24,32},{32,40},{40,48},{48,56},{1,9},{9,17},... | collective-permute-start | bytes 49160 | tf_op jit(solution)/shard_map/ppermute | solution.py:36
  160.6 4.5 %collective-permute-start.15 = (bf16[1,1,16,512]{3,2,1,0:T(8,128)(2,1)S(1)}, bf16[1,1,16,512]{3,2,1,0:T(8,128)(2,1)S(1)}, u32[]{:S(2)}, u32[]{:S(2)}) collective-permute-start(bf16[1,1,16,512]{3,2,1,0:T(8,128)(2,1)S(1)} %get-tuple-element.43), channel_id=1, source_target_pairs={{8,0},{16,8},{24,16},{32,24},{40,32},{48,40},{56,48},{9,1},{17,9},... | collective-permute-start | bytes 49160 | tf_op jit(solution)/shard_map/ppermute | solution.py:39
  167.4 9.7 %collective-permute-start.16 = (bf16[1,24,1,16]{1,3,2,0:T(8,128)(2,1)S(1)}, bf16[1,24,1,16]{1,3,2,0:T(8,128)(2,1)S(1)}, u32[]{:S(2)}, u32[]{:S(2)}) collective-permute-start(bf16[1,24,1,16]{1,3,2,0:T(8,128)(2,1)S(1)} %get-tuple-element.50), channel_id=1, source_target_pairs={{0,8},{8,16},{16,24},{24,32},{32,40},{40,48},{48,56},{1,9},{9,17},... | collective-permute-start | bytes 2312 | tf_op jit(solution)/shard_map/ppermute | solution.py:36
  170.8 6.3 %collective-permute-start.17 = (bf16[1,24,1,16]{1,3,2,0:T(8,128)(2,1)S(1)}, bf16[1,24,1,16]{1,3,2,0:T(8,128)(2,1)S(1)}, u32[]{:S(2)}, u32[]{:S(2)}) collective-permute-start(bf16[1,24,1,16]{1,3,2,0:T(8,128)(2,1)S(1)} %get-tuple-element.51), channel_id=1, source_target_pairs={{8,0},{16,8},{24,16},{32,24},{40,32},{48,40},{56,48},{9,1},{17,9},... | collective-permute-start | bytes 2312 | tf_op jit(solution)/shard_map/ppermute | solution.py:39
  178.6 21.8 %collective-permute-start.18 = (bf16[1,1,16,512]{3,2,1,0:T(8,128)(2,1)S(1)}, bf16[1,1,16,512]{3,2,1,0:T(8,128)(2,1)S(1)}, u32[]{:S(2)}, u32[]{:S(2)}) collective-permute-start(bf16[1,1,16,512]{3,2,1,0:T(8,128)(2,1)S(1)} %get-tuple-element.40), channel_id=1, source_target_pairs={{0,8},{8,16},{16,24},{24,32},{32,40},{40,48},{48,56},{1,9},{9,17},... | collective-permute-start | bytes 49160 | tf_op jit(solution)/shard_map/ppermute | solution.py:36
  182.6 17.8 %collective-permute-start.19 = (bf16[1,1,16,512]{3,2,1,0:T(8,128)(2,1)S(1)}, bf16[1,1,16,512]{3,2,1,0:T(8,128)(2,1)S(1)}, u32[]{:S(2)}, u32[]{:S(2)}) collective-permute-start(bf16[1,1,16,512]{3,2,1,0:T(8,128)(2,1)S(1)} %get-tuple-element.41), channel_id=1, source_target_pairs={{8,0},{16,8},{24,16},{32,24},{40,32},{48,40},{56,48},{9,1},{17,9},... | collective-permute-start | bytes 49160 | tf_op jit(solution)/shard_map/ppermute | solution.py:39
  184.6 14.6 %all-to-all-start.1 = ((f32[8,1,1]{2,1,0:T(1,128)}), f32[8,1,1]{2,1,0:T(1,128)S(1)}, u32[]{:S(2)}, u32[]{:S(2)}) async-start(f32[8,1,1]{2,1,0:T(1,128)} %copy.48), calls=%async_computation.1 | async-start | bytes 8192 | tf_op jit(solution)/shard_map/all_to_all | solution.py:52
  206.4 13.4 %all-to-all-start.2 = ((f32[8,1,1]{2,1,0:T(1,128)}), f32[8,1,1]{2,1,0:T(1,128)S(1)}, u32[]{:S(2)}, u32[]{:S(2)}) async-start(f32[8,1,1]{2,1,0:T(1,128)} %broadcast_in_dim.91), calls=%async_computation.2 | async-start | bytes 8192 | tf_op jit(solution)/shard_map/all_to_all | solution.py:58
  (14 other events, 173.2 us)
where the time goes:
time: 226 us; the launch traced here: 222 us
  starting transfers between devices  84.2 us (37%)
  waiting for transfers between devices  60.7 us (27%)
  matrix products  47.6 us (21%)
  between operations  12.4 us (5%)
  other arithmetic  11.4 us (5%)
  local copies, waits for them, and re-layouts  5.92 us (3%)
    ppermute x6, waiting for transfers between devices, padded_2(): lax.ppermute(first, axis, [(b, a) for a, b in up])  34.4 us
    dot_general x45, matrix products, conv_out(): jnp.einsum('bhwc,co->bohw', window, weights[tap_idx], preferred_element_t...  30.4 us
    ppermute x4, starting transfers between devices, with_halo(): lax.ppermute(lax.slice_in_dim(block, block.shape[dim] - width, None, axis...  25 us
    ppermute x6, starting transfers between devices, padded_2(): lax.ppermute(first, axis, [(b, a) for a, b in up])  16.1 us
    ppermute x6, starting transfers between devices, padded_2(): lax.ppermute(last, axis, up)  15.6 us
    dot_general x40, matrix products, conv_in(): jnp.einsum('bchw,co->bhwo', window, weights[tap_idx], preferred_element_t...  10.6 us
    all_to_all x1, starting transfers between devices, body(): lax.all_to_all(kept_chan, 'chan', split_axis=0, concat_axis=2, tiled=True)  7.84 us
    all_to_all x1, starting transfers between devices, summed_on_arrival(): pieces = lax.all_to_all(in_blocks(x, dim, length), axis, 0, 0, tiled=True)  7.61 us
  transfers between devices with their start and end apart: 23, of which 13 were waited for; matrix products, arithmetic and copies ran while one was open for 3% of the time, Pallas kernels for 0%

commit v1 on v0

v1 whole, which is shorter than its diff:
```python
import math

import jax
import jax.numpy as jnp
from jax import lax
from jax.experimental import pallas as pl
from jax.experimental.pallas import tpu as pltpu
from jax.sharding import PartitionSpec as P

MESH = pl.DeviceIdType.MESH
F32 = jnp.float32
BF16 = jnp.bfloat16
LOG_TWO_PI = math.log(2.0 * math.pi)

HID = 512
ROWS = 8
CHAN = 8
C2, C3 = 24, 48
STEPS2, STEPS3 = 3, 2
COLS = 32
LANES = 128
REACH = 2
BLOCKS = 2 * REACH + 1
WIDE = BLOCKS * 8 * COLS
NARROW = WIDE - 2 * LANES
KMID = 160
KTOP = 224
NTOP = 256
DIMS = 24 * 64 * 32


def iota(shape, dim):
    return lax.broadcasted_iota(jnp.int32, shape, dim)


def dot(a, b):
    return jnp.dot(a, b, preferred_element_type=F32)


def exact_dot(a, b):
    return jnp.dot(a, b, preferred_element_type=F32, precision=lax.Precision.HIGHEST)


def column(row):
    n = row.shape[1]
    eye = iota((n, n), 0) == iota((n, n), 1)
    return jnp.sum(jnp.where(eye, row, 0.0), axis=1, keepdims=True)


def place_mid(n, dim):
    at = iota((n, n), dim)
    return jnp.where(at < 12, at, jnp.where(at < 16, at + 8, at - 4))


def mixing(shift, gain, lower, upper, diag):
    n = shift.shape[1]
    i, j = iota((n, n), 0), iota((n, n), 1)
    low = jnp.where(j < i, lower, 0.0) + jnp.where(i == j, 1.0, 0.0)
    up = jnp.where(j > i, upper, 0.0) + jnp.where(i == j, jnp.exp(diag), 0.0)
    a = exact_dot(low, up) * jnp.exp(gain)
    return a, jnp.sum(a * shift, axis=1, keepdims=True)


def stacked(a, b, width, bias_at):
    rows, n = a.shape
    if width > n:
        a = jnp.concatenate([a, jnp.zeros((rows, width - n), F32)], axis=1)
    a = jnp.where(iota((rows, width), 1) == bias_at, b, a)
    high = a.astype(BF16).astype(F32)
    low = a - high
    return jnp.concatenate([high, high, low], axis=1).astype(BF16)


def split_mix(a, v):
    high = v.astype(BF16)
    low = (v - high.astype(F32)).astype(BF16)
    return dot(a, jnp.concatenate([high, low, high], axis=0))


def roll(x, by):
    n = x.shape[1]
    by = by % n
    return x if by == 0 else pltpu.roll(x, by, 1)


def ones_block(n, height, at):
    return jnp.where(iota((height, n), 0) == at, 1.0, 0.0)


def conditioner(q, inside, width, w1, w2, b2, w3, b3):
    n = q.shape[1]
    col = iota((1, n), 1) % width
    from_left, from_right = col > 0, col < width - 1
    left = jnp.where(from_left, roll(q, 1), 0.0)
    right = jnp.where(from_right, roll(q, -1), 0.0)
    taps = [roll(side, -width * dy) for dy in (-1, 0, 1) for side in (left, q, right)]
    taps.append(ones_block(n, w1.shape[1] - 9 * q.shape[0], 0))
    patches = jnp.concatenate(taps, axis=0).astype(BF16)
    pieces = []
    for at in range(0, n, 256):
        h1 = jnp.maximum(dot(w1[...], patches[:, at : at + 256]), 0.0).astype(BF16)
        bias = jnp.concatenate([b2[...]] * 2, axis=1)
        h2 = jnp.maximum(dot(w2[...], h1) + bias, 0.0).astype(BF16)
        pieces.append(dot(w3[...], h2))
    z = pieces[0] if len(pieces) == 1 else jnp.concatenate(pieces, axis=1)
    z = jnp.where(inside, z, 0.0)
    outs = w3.shape[0] // 9
    sides = []
    for dx in range(3):
        total = z[(3 + dx) * outs : (4 + dx) * outs]
        total += roll(z[dx * outs : (dx + 1) * outs], width)
        total += roll(z[(6 + dx) * outs : (7 + dx) * outs], -width)
        sides.append(total)
    out = sides[1] + jnp.where(from_left, roll(sides[0], 1), 0.0)
    out += jnp.where(from_right, roll(sides[2], -1), 0.0)
    return out + b3


def gate(g):
    small = jnp.exp(-jnp.abs(g))
    sigmoid = jnp.where(g >= 0.0, 1.0, small) / (1.0 + small)
    return sigmoid, jnp.minimum(g, 0.0) - jnp.log(1.0 + small)


def kernel(
    images,
    shift_mid,
    gain_mid,
    lower_mid,
    upper_mid,
    diag_mid,
    first_mid,
    first_bias_mid,
    second_mid,
    second_bias_mid,
    third_mid,
    third_bias_mid,
    shift_top,
    gain_top,
    lower_top,
    upper_top,
    diag_top,
    first_top,
    first_bias_top,
    second_top,
    second_bias_top,
    third_top,
    third_bias_top,
    latent_mid,
    latent_top,
    loglik,
    pictures,
    packed,
    arrived,
    first2,
    second2,
    third2,
    first3,
    second3,
    third3,
    small2,
    small3,
    mix2,
    mix3,
    bias2,
    bias3,
    tall,
    w1_mid,
    w2_mid,
    b2_mid,
    w3_mid,
    w1_top,
    w2_top,
    b2_top,
    w3_top,
    sent_latent,
    got_latent,
    terms,
    load_sem,
    small_sem,
    weight_sem,
    send_sem,
    recv_sem,
    latent_send,
    latent_recv,
    term_send,
    term_recv,
):
    r, c = lax.axis_index("rows"), lax.axis_index("chan")
    barrier = pltpu.get_barrier_semaphore()

    picture_load = pltpu.make_async_copy(images, pictures, load_sem)
    picture_load.start()
    given2 = (shift_mid, gain_mid, lower_mid, upper_mid, diag_mid, first_bias_mid, second_bias_mid, third_bias_mid)
    given3 = (shift_top, gain_top, lower_top, upper_top, diag_top, first_bias_top, second_bias_top, third_bias_top)
    small_loads = [
        pltpu.make_async_copy(src, dst, small_sem.at[i])
        for i, (src, dst) in enumerate(zip(given2 + given3, small2 + small3))
    ]
    for load in small_loads:
        load.start()
    weight_loads = []
    for s in range(STEPS2):
        for src, dst in ((second_mid, second2), (first_mid, first2), (third_mid, third2)):
            weight_loads.append(
                pltpu.make_async_copy(src.at[s], dst.at[s], weight_sem.at[len(weight_loads)])
            )
    for s in range(STEPS3):
        for src, dst in ((second_top, second3), (first_top, first3), (third_top, third3)):
            weight_loads.append(
                pltpu.make_async_copy(src.at[s], dst.at[s], weight_sem.at[len(weight_loads)])
            )
    for load in weight_loads:
        load.start()

    def in_image(d, body):
        if d == 0:
            body()
        else:
            pl.when((r + d >= 0) & (r + d < ROWS))(body)

    near = range(-REACH, REACH + 1)

    arrived[...] = jnp.zeros_like(arrived)
    for d in near:

        def greet(d=d):
            for k in range(1 if d == 0 else 0, CHAN):
                pl.semaphore_signal(
                    barrier, 1, device_id={"rows": r + d, "chan": (c + k) % CHAN}, device_id_type=MESH
                )

        in_image(d, greet)
    for d in range(REACH + 1, ROWS):
        for far in (-d, d):

            def greet_far(far=far):
                pl.semaphore_signal(barrier, 1, device_id={"rows": r + far}, device_id_type=MESH)

            in_image(far, greet_far)

    picture_load.wait()
    group = iota((8, LANES), 1) // COLS
    for i in range(8):
        tile = jnp.zeros((8, LANES), F32)
        for k in range(3):
            part = pictures[i, 8 * k : 8 * k + 8, :]
            part = jnp.concatenate([part, jnp.zeros((8, LANES - COLS), F32)], axis=1)
            tile = jnp.where(group == k, roll(part, COLS * k), tile)
        packed[i] = tile

    def prepare_small():
        for load in small_loads:
            load.wait()
        shift, gain, lower, upper, diag, _, second_b, third_b = small2
        for s in range(STEPS2):
            a, b = mixing(shift[s : s + 1], gain[s : s + 1], lower[s], upper[s], diag[s : s + 1])
            to_rows = jnp.where(place_mid(C2, 0) == iota((C2, C2), 1), 1.0, 0.0)
            a = exact_dot(to_rows, a)
            if s:
                to_columns = jnp.where(place_mid(C2, 1) == iota((C2, C2), 0), 1.0, 0.0)
                a = exact_dot(a, to_columns)
            b = exact_dot(to_rows, b)
            mix2[s] = stacked(a, b, 32, C2)
            extra = third_b[s : s + 1] + jnp.where(iota((1, C2), 1) < C2 // 2, 2.0, 0.0)
            bias2[s] = jnp.sum(to_rows * extra, axis=1, keepdims=True)
            b2_mid[s] = jnp.broadcast_to(second_b[s : s + 1], (LANES, HID)).T
        shift, gain, lower, upper, diag, _, second_b, third_b = small3
        for s in range(STEPS3):
            a, b = mixing(shift[s : s + 1], gain[s : s + 1], lower[s], upper[s], diag[s : s + 1])
            if s == 0:
                n, k = iota((C3, 64), 0), iota((C3, 64), 1)
                row = n // 4
                at = (n % 4) * 16 + jnp.where(row < 8, row, row + 4)
                a = exact_dot(a, jnp.where(at == k, 1.0, 0.0))
                mix3[s] = stacked(a, b, 80, 64)
            else:
                mix3[s] = stacked(a, b, 80, C3)
            extra = third_b[s : s + 1] + jnp.where(iota((1, C3), 1) < C3 // 2, 2.0, 0.0)
            bias3[s] = column(extra)
            b2_top[s] = jnp.broadcast_to(second_b[s : s + 1], (LANES, HID)).T

    def prepare_mid(s):
        for i in range(3):
            weight_loads[3 * s + i].wait()
        w2_mid[s] = second2[s].T
        tall[...] = jnp.zeros_like(tall)
        for t in range(9):
            tall[16 * t : 16 * t + 12, :] = first2[s, t].astype(F32)
        tall[144:145, :] = small2[5][s : s + 1].astype(F32)
        w1_mid[s] = tall[:KMID, :].T.astype(BF16)
        to_rows = jnp.where(place_mid(C2, 0) == iota((C2, C2), 1), 1.0, 0.0).astype(BF16)
        for t in range(9):
            w3_mid[s, C2 * t : C2 * (t + 1), :] = dot(to_rows, third2[s, t]).astype(BF16)

    def prepare_top(s):
        for i in range(3):
            weight_loads[3 * STEPS2 + 3 * s + i].wait()
        w2_top[s] = second3[s].T
        for t in range(9):
            tall[24 * t : 24 * (t + 1), :] = first3[s, t].astype(F32)
            w3_top[s, C3 * t : C3 * (t + 1), :] = third3[s, t]
        tall[216:217, :] = small3[5][s : s + 1].astype(F32)
        tall[217:, :] = jnp.zeros((KTOP - 217, HID), F32)
        w1_top[s] = tall[...].T.astype(BF16)

    prepare_small()
    prepare_mid(0)

    for edge in range(REACH + 1):
        blocks = REACH + 1 + edge

        def meet(blocks=blocks):
            pl.semaphore_wait(barrier, CHAN * blocks - 1 + ROWS - blocks)

        if edge < REACH:
            pl.when((r == edge) | (r == ROWS - 1 - edge))(meet)
        else:
            pl.when((r >= edge) & (r <= ROWS - 1 - edge))(meet)

    def row_copy(d, k):
        to = (c + k) % CHAN
        return pltpu.make_async_remote_copy(
            src_ref=packed.at[to],
            dst_ref=arrived.at[8 * (REACH - d) + c],
            send_sem=send_sem,
            recv_sem=recv_sem.at[REACH - d],
            device_id={"rows": r + d, "chan": to},
            device_id_type=MESH,
        )

    def sends(d, body):
        if d == REACH:
            pl.when((r + d < ROWS) & (c >= 2))(body)
        elif d == -REACH:
            pl.when((r + d >= 0) & (c < CHAN - 2))(body)
        else:
            in_image(d, body)

    for d in sorted(near, key=lambda d: -abs(d)):

        def send(d=d):
            for k in range(1 if d == 0 else 0, CHAN):
                row_copy(d, k).start()

        sends(d, send)
    arrived[8 * REACH + c] = packed[c]

    for s in range(1, STEPS2):
        prepare_mid(s)
    for s in range(STEPS3):
        prepare_top(s)

    for d in near:

        def receive(d=d):
            first, last = 8 * (d + REACH), 8 * (d + REACH) + 8
            if d == -REACH:
                first += 2
            elif abs(d) == REACH:
                last -= 2
            elif d == 0:
                last -= 1
            tiles = arrived.at[pl.ds(first, last - first)]
            pltpu.make_async_copy(tiles, tiles, recv_sem.at[d + REACH]).wait()

        in_image(d, receive)

    rows_of_lanes = []
    for k in range(3):
        lanes_of_k = []
        for g in range(WIDE // LANES):
            tile = None
            for j in range(4):
                part = roll(arrived[4 * g + j], COLS * (j - k))
                tile = part if tile is None else jnp.where(group == j, part, tile)
            lanes_of_k.append(tile)
        rows_of_lanes.append(jnp.concatenate(lanes_of_k, axis=1))
    state = jnp.concatenate(rows_of_lanes + [ones_block(WIDE, 8, 0)], axis=0)

    own = slice(NARROW // 2 - LANES, NARROW // 2 + LANES)
    loglik_terms = jnp.zeros((16, 2 * LANES), F32)
    for s in range(STEPS2):
        n = WIDE if s == 0 else NARROW
        row = iota((1, n), 1) // COLS + (0 if s == 0 else 4) + 8 * (r - REACH)
        inside = (row >= 0) & (row < 8 * ROWS)
        u = split_mix(mix2[s], state)
        q = jnp.where(inside, u[:16], 0.0)
        out = conditioner(
            q, inside, COLS, w1_mid.at[s], w2_mid.at[s], b2_mid.at[s], w3_mid.at[s], bias2[s]
        )
        if s == 0:
            u, out = u[:, LANES:-LANES], out[:, LANES:-LANES]
        sigmoid, log_sigmoid = gate(out[:16])
        loglik_terms += jnp.where(iota((16, 2 * LANES), 0) < 12, log_sigmoid[:, own], 0.0)
        lower_half = iota((8, 1), 0) < 4
        mixed = (u[8:16] + out[8:16]) * pltpu.roll(sigmoid[8:16], 4, 0)
        mixed = jnp.where(lower_half, u[8:16], mixed)
        rest = (u[16:24] + out[16:24]) * sigmoid[:8]
        state = jnp.concatenate([u[:8], mixed, rest, ones_block(NARROW, 8, 0)], axis=0)

    latent = state[:16, own]
    loglik_terms -= jnp.where(iota((16, 2 * LANES), 0) < 12, 0.5 * latent * latent, 0.0)
    for half in range(2):
        sent_latent[half] = latent[:, LANES * half : LANES * (half + 1)]

    kept = jnp.concatenate([state[16:24], state[8:16]], axis=0)
    lane, to = iota((2 * LANES, 2 * LANES), 0), iota((2 * LANES, 2 * LANES), 1)
    p, col = lane // COLS, lane % COLS
    place = (2 * (p % 2) + col % 2) * 64 + (p // 2) * 16 + col // 2
    permutation = jnp.where(place == to, 1.0, 0.0).astype(BF16)
    streams = []
    for block in range(3):
        rest = kept[:, LANES * (1 + 2 * block) : LANES * (3 + 2 * block)]
        for _ in range(3):
            high = rest.astype(BF16)
            streams.append(high)
            rest = rest - high.astype(F32)
    moved = dot(jnp.concatenate(streams, axis=0), permutation)
    blocks = [
        moved[48 * b : 48 * b + 16] + moved[48 * b + 16 : 48 * b + 32] + moved[48 * b + 32 : 48 * b + 48]
        for b in range(3)
    ]
    lane64 = iota((16, LANES), 1) < 64
    squeezed = []
    for ij in range(4):
        half = LANES * (ij // 2)
        at = [b[:, half : half + LANES] for b in blocks]
        if ij % 2 == 0:
            left, right = jnp.where(lane64, at[0], roll(at[1], 64)), at[2]
        else:
            left, right = jnp.where(lane64, roll(at[0], 64), at[1]), roll(at[2], 64)
        squeezed.append(jnp.concatenate([left, right], axis=1))
    state = jnp.concatenate(squeezed + [ones_block(NTOP, 16, 0)], axis=0)

    def latent_copy(k):
        to = (c + k) % CHAN
        return pltpu.make_async_remote_copy(
            src_ref=sent_latent.at[to // 4],
            dst_ref=got_latent.at[c],
            send_sem=latent_send,
            recv_sem=latent_recv,
            device_id={"chan": to},
            device_id_type=MESH,
        )

    for k in range(1, CHAN):
        latent_copy(k).start()
    got_latent[c] = sent_latent[c // 4]

    row = iota((1, NTOP), 1) // 16
    inside = (row + 4 * r >= 4) & (row + 4 * r < 4 * ROWS + 4) & (row < 12)
    own_top = (iota((1, LANES), 1) >= 64)
    top_terms = jnp.zeros((24, LANES), F32)
    for s in range(STEPS3):
        u = split_mix(mix3[s], state)
        q = jnp.where(inside, u[:24], 0.0)
        out = conditioner(
            q, inside, 16, w1_top.at[s], w2_top.at[s], b2_top.at[s], w3_top.at[s], bias3[s]
        )
        sigmoid, log_sigmoid = gate(out[:24])
        top_terms += log_sigmoid[:, :LANES]
        rest = (u[24:] + out[24:]) * sigmoid
        state = jnp.concatenate([u[:24], rest, ones_block(NTOP, 32, 0)], axis=0)
    z = state[:C3, :LANES]
    squares = z * z
    top_terms = jnp.where(own_top, top_terms - 0.5 * (squares[:24] + squares[24:]), 0.0)

    logdets = 256.0 * (jnp.sum(small2[1][...]) + jnp.sum(small2[4][...]))
    logdets += 64.0 * (jnp.sum(small3[1][...]) + jnp.sum(small3[4][...]))
    total = jnp.sum(loglik_terms) + jnp.sum(top_terms) + logdets
    total = (total - 0.5 * LOG_TWO_PI * (12 * 256 + 48 * 64)) * (1.0 / DIMS)
    terms[r] = jnp.full((1, LANES), total, F32)

    def term_copy(k):
        return pltpu.make_async_remote_copy(
            src_ref=terms.at[r],
            dst_ref=terms.at[r],
            send_sem=term_send,
            recv_sem=term_recv,
            device_id={"rows": (r + k) % ROWS},
            device_id_type=MESH,
        )

    for k in range(1, ROWS):
        term_copy(k).start()

    latent_top[0] = z.T[64:].reshape(4, 16, C3)

    others = got_latent.at[pl.ds(0, CHAN - 1)]
    pltpu.make_async_copy(others, others, latent_recv).wait()
    for i in range(8):
        turned = pltpu.roll(got_latent[i], (LANES - COLS * (c % 4)) % LANES, 1)
        latent_mid[i] = turned[:12, :COLS]

    others = terms.at[pl.ds(0, ROWS - 1)]
    pltpu.make_async_copy(others, others, term_recv).wait()
    whole = terms[0]
    for i in range(1, ROWS):
        whole = whole + terms[i]
    loglik[...] = whole

    pltpu.make_async_copy(others, others, term_send).wait()
    others = got_latent.at[pl.ds(0, CHAN - 1)]
    pltpu.make_async_copy(others, others, latent_send).wait()
    for d in near:

        def left_here(d=d):
            tiles = packed.at[pl.ds(0, CHAN - 1 if d == 0 else CHAN)]
            pltpu.make_async_copy(tiles, tiles, send_sem).wait()

        sends(d, left_here)


def body(*given):
    given = list(given)
    given[0] = given[0].reshape(8, C2, COLS)
    given[10] = given[10].transpose(0, 1, 3, 2)
    given[21] = given[21].transpose(0, 1, 3, 2)

    def small(n, steps):
        return (
            pltpu.VMEM((steps, n), F32),
            pltpu.VMEM((steps, n), F32),
            pltpu.VMEM((steps, n, n), F32),
            pltpu.VMEM((steps, n, n), F32),
            pltpu.VMEM((steps, n), F32),
            pltpu.VMEM((steps, HID), BF16),
            pltpu.VMEM((steps, HID), F32),
            pltpu.VMEM((steps, n), F32),
        )

    latent_mid, latent_top, loglik = pl.pallas_call(
        kernel,
        out_shape=(
            jax.ShapeDtypeStruct((8, 12, COLS), F32),
            jax.ShapeDtypeStruct((1, 4, 16, C3), F32),
            jax.ShapeDtypeStruct((1, LANES), F32),
        ),
        in_specs=[pl.BlockSpec(memory_space=pl.ANY)] * 23,
        out_specs=tuple(pl.BlockSpec(memory_space=pltpu.VMEM) for _ in range(3)),
        scratch_shapes=[
            pltpu.VMEM((8, C2, COLS), F32),
            pltpu.VMEM((8, 8, LANES), F32),
            pltpu.VMEM((8 * BLOCKS, 8, LANES), F32),
            pltpu.VMEM((STEPS2, 9, 12, HID), BF16),
            pltpu.VMEM((STEPS2, HID, HID), BF16),
            pltpu.VMEM((STEPS2, 9, C2, HID), BF16),
            pltpu.VMEM((STEPS3, 9, 24, HID), BF16),
            pltpu.VMEM((STEPS3, HID, HID), BF16),
            pltpu.VMEM((STEPS3, 9, C3, HID), BF16),
            small(C2, STEPS2),
            small(C3, STEPS3),
            pltpu.VMEM((STEPS2, C2, 96), BF16),
            pltpu.VMEM((STEPS3, C3, 240), BF16),
            pltpu.VMEM((STEPS2, C2, 1), F32),
            pltpu.VMEM((STEPS3, C3, 1), F32),
            pltpu.VMEM((KTOP, HID), F32),
            pltpu.VMEM((STEPS2, HID, KMID), BF16),
            pltpu.VMEM((STEPS2, HID, HID), BF16),
            pltpu.VMEM((STEPS2, HID, LANES), F32),
            pltpu.VMEM((STEPS2, 9 * C2, HID), BF16),
            pltpu.VMEM((STEPS3, HID, KTOP), BF16),
            pltpu.VMEM((STEPS3, HID, HID), BF16),
            pltpu.VMEM((STEPS3, HID, LANES), F32),
            pltpu.VMEM((STEPS3, 9 * C3, HID), BF16),
            pltpu.VMEM((2, 16, LANES), F32),
            pltpu.VMEM((CHAN, 16, LANES), F32),
            pltpu.VMEM((ROWS, 1, LANES), F32),
            pltpu.SemaphoreType.DMA,
            pltpu.SemaphoreType.DMA((16,)),
            pltpu.SemaphoreType.DMA((15,)),
            pltpu.SemaphoreType.DMA,
            pltpu.SemaphoreType.DMA((BLOCKS,)),
            pltpu.SemaphoreType.DMA,
            pltpu.SemaphoreType.DMA,
            pltpu.SemaphoreType.DMA,
            pltpu.SemaphoreType.DMA,
        ],
        compiler_params=pltpu.CompilerParams(collective_id=0, has_side_effects=True, vmem_limit_bytes=60 * 2**20),
    )(*given)
    return (
        latent_mid.reshape(8, 12, 1, COLS),
        latent_top.transpose(0, 3, 1, 2),
        loglik[0, :1],
    )


def solution(mesh):
    placed = (P("batch", None, ("rows", "chan"), None),) + (P(),) * 22
    return jax.shard_map(
        body,
        mesh=mesh,
        in_specs=placed,
        out_specs=(
            P("batch", None, ("rows", "chan"), None),
            P(("batch", "chan"), None, "rows", None),
            P(("batch", "chan")),
        ),
        check_vma=False,
    )
```

time: 226 us -> 46.2 us (0.20); the launches traced: 222 us -> 45.9 us
  starting transfers between devices: 84.2 us -> 0 us
  waiting for transfers between devices: 60.7 us -> 0 us
  matrix products: 47.6 us -> 0 us
  Pallas kernels: 0 us -> 40.6 us
  other arithmetic: 11.4 us -> 0 us
  between operations: 12.4 us -> 2.47 us
  local copies, waits for them, and re-layouts: 5.92 us -> 2.88 us
    ppermute x20 -> x0, starting transfers between devices: 61.9 us -> none  [the longest x4 25 us: with_halo(): lax.ppermute(lax.slice_in_dim(block, block.shape[dim] - width, None, axis...]
    dot_general x100 -> x0, matrix products: 47.6 us -> none  [the longest x45 30.4 us: conv_out(): jnp.einsum('bhwc,co->bohw', window, weights[tap_idx], preferred_element_t...]
    ppermute x20 -> x0, waiting for transfers between devices: 41 us -> none  [the longest x6 34.4 us: padded_2(): lax.ppermute(first, axis, [(b, a) for a, b in up])]
    pallas_call x0 -> x1, Pallas kernels: none -> 40.6 us  [body(): pl.pallas_call(kernel, out_shape=(jax.ShapeDtypeStruct((8, 12, COLS), F32...]
    all_to_all x3 -> x0, starting transfers between devices: 22.3 us -> none  [the longest x1 7.84 us: body(): lax.all_to_all(kept_chan, 'chan', split_axis=0, concat_axis=2, tiled=True)]
    all_to_all x3 -> x0, waiting for transfers between devices: 19.7 us -> none  [the longest x1 6.96 us: summed_on_arrival(): pieces = lax.all_to_all(in_blocks(x, dim, length), axis, 0, 0, tiled=True)]
    reduce_sum x10 -> x0, other arithmetic: 6.51 us -> none  [the longest x2 2.19 us: flow_step(): jnp.sum(diag_log)]
  transfers between devices with their start and end apart: 23 -> 0, of which waited for: 13 -> 0; matrix products, arithmetic and copies ran while one was open for 3% -> 0% of each run, Pallas kernels for 0% -> 0%
where the time goes in v1:
time: 46.2 us; the launch traced here: 45.9 us
  Pallas kernels  40.6 us (88%)
  local copies, waits for them, and re-layouts  2.88 us (6%)
  between operations  2.47 us (5%)
    pallas_call x1, Pallas kernels, body(): pl.pallas_call(kernel, out_shape=(jax.ShapeDtypeStruct((8, 12, COLS), F32...  40.6 us
    unnamed x2, local copies, waits for them, and re-layouts  2.88 us

profile of v1, /device:TPU:1, one launch (start us, length us, event | category | flops | bytes accessed | tf_op | source)
XLA Modules:
  0.0 45.9 jit_solution(4741443144757415488)
XLA Ops:
  0.6 40.6 %shard_map.238 = (f32[8,12,32]{2,1,0:T(8,128)}, f32[1,4,16,48]{3,2,1,0:T(8,128)}, f32[1,128]{1,0:T(1,128)}) custom-call(f32[8,24,32]{2,1,0:T(8,128)} %bitcast.9, f32[3,24]{1,0:T(4,128)} %shift_mid.1, f32[3,24]{1,0:T(4,128)} %gain_mid.1, f32[3,24,24]{2,1,0:T(8,128)} %lower_mid.1, f32[3,24,24]{2,1,0:T(8,128)} %upper_mid.1, f32[3,24]{1,0:T(4,128)} %diag_mid.1, ...), custom_call_target="tpu_custom_call" | custom-call | tf_op jit(solution)/shard_map/pallas_call | solution.py:533
  41.2 1.5 %copy.26 = f32[8,12,1,32]{3,2,1,0:T(1,128)} copy(f32[8,12,1,32]{3,1,0,2:T(8,128)} %bitcast.10) | data formatting | bytes 24576
  42.7 1.4 %copy.29 = f32[1,48,4,16]{1,3,2,0:T(8,128)} copy(f32[1,48,4,16]{1,3,2,0:T(8,128)} %bitcast.11) | data formatting | bytes 24576

commit v2 on v1

--- a/solution.py
+++ b/solution.py
@@ -87,39 +87,129 @@
     return jnp.where(iota((height, n), 0) == at, 1.0, 0.0)
 
 
-def conditioner(q, inside, width, w1, w2, b2, w3, b3):
-    n = q.shape[1]
-    col = iota((1, n), 1) % width
-    from_left, from_right = col > 0, col < width - 1
-    left = jnp.where(from_left, roll(q, 1), 0.0)
-    right = jnp.where(from_right, roll(q, -1), 0.0)
-    taps = [roll(side, -width * dy) for dy in (-1, 0, 1) for side in (left, q, right)]
-    taps.append(ones_block(n, w1.shape[1] - 9 * q.shape[0], 0))
-    patches = jnp.concatenate(taps, axis=0).astype(BF16)
-    pieces = []
-    for at in range(0, n, 256):
-        h1 = jnp.maximum(dot(w1[...], patches[:, at : at + 256]), 0.0).astype(BF16)
-        bias = jnp.concatenate([b2[...]] * 2, axis=1)
-        h2 = jnp.maximum(dot(w2[...], h1) + bias, 0.0).astype(BF16)
-        pieces.append(dot(w3[...], h2))
-    z = pieces[0] if len(pieces) == 1 else jnp.concatenate(pieces, axis=1)
-    z = jnp.where(inside, z, 0.0)
-    outs = w3.shape[0] // 9
-    sides = []
-    for dx in range(3):
-        total = z[(3 + dx) * outs : (4 + dx) * outs]
-        total += roll(z[dx * outs : (dx + 1) * outs], width)
-        total += roll(z[(6 + dx) * outs : (7 + dx) * outs], -width)
-        sides.append(total)
-    out = sides[1] + jnp.where(from_left, roll(sides[0], 1), 0.0)
-    out += jnp.where(from_right, roll(sides[2], -1), 0.0)
-    return out + b3
+def turned(x, by):
+    return pltpu.roll(x, -by % LANES, 1)
+
+
+def moved(blocks, j, by, lane):
+    if by == 0:
+        return blocks(j, 0)
+    here, beside = blocks(j, by), blocks(j + (1 if by > 0 else -1), by)
+    if beside is None:
+        return here
+    return jnp.where(lane < LANES - by, here, beside) if by > 0 else jnp.where(lane >= -by, here, beside)
+
+
+def cached(get):
+    kept = {}
+
+    def blocks(j, by):
+        if (j, by) not in kept:
+            x = get(j)
+            kept[j, by] = x if x is None or by == 0 else turned(x, by)
+        return kept[j, by]
+
+    return blocks
+
+
+class Step:
+    def __init__(self, first, last, width, half, inside, mix, w1, w2, b2, w3, b3, scratch):
+        self.first, self.last, self.width, self.half = first, last, width, half
+        self.inside, self.mix_w, self.w1, self.w2, self.b2, self.w3, self.b3 = inside, mix, w1, w2, b2, w3, b3
+        self.patches, self.h1, self.h2, self.z = scratch
+        self.outs = w3.shape[0] // 9
+        self.u, self.q = {}, {}
+        self.lane = iota((1, LANES), 1)
+        col = self.lane % width
+        self.edge = {-1: col > 0, 1: col < width - 1}
+        self.q_blocks = cached(lambda j: self.q.get(j))
+        self.z_blocks = [
+            cached(lambda j, t=t: self.z_block(t, j)) for t in range(9)
+        ]
+
+    def tiles(self):
+        return (self.last - self.first) // 2
+
+    def pair(self, t):
+        return self.first + 2 * t, self.first + 2 * t + 1
+
+    def lanes(self, t):
+        return slice(2 * LANES * t, 2 * LANES * (t + 1))
+
+    def mix(self, t, state):
+        pair = self.pair(t)
+        u = split_mix(self.mix_w[...], jnp.concatenate([state(j) for j in pair], axis=1))
+        rows = 16 if self.half == 12 else 24
+        for i, j in enumerate(pair):
+            self.u[j] = u[:, LANES * i : LANES * (i + 1)]
+            self.q[j] = jnp.where(self.inside(j), self.u[j][:rows], 0.0)
+            if rows == 16:
+                self.q[j] = self.q[j].astype(BF16)
+
+    def patch(self, t):
+        taps = []
+        for dy in (-1, 0, 1):
+            for dx in (-1, 0, 1):
+                parts = []
+                for j in self.pair(t):
+                    part = moved(self.q_blocks, j, self.width * dy + dx, self.lane)
+                    parts.append(jnp.where(self.edge[dx], part, jnp.zeros_like(part)) if dx else part)
+                taps.append(jnp.concatenate(parts, axis=1))
+        if self.half == 12:
+            for i, tap in enumerate(taps):
+                self.patches[16 * i : 16 * (i + 1), self.lanes(t)] = tap
+        else:
+            taps.append(ones_block(2 * LANES, 8, 0))
+            self.patches[:, self.lanes(t)] = jnp.concatenate(taps, axis=0).astype(BF16)
+
+    def one(self, t):
+        self.h1[:, self.lanes(t)] = jnp.maximum(dot(self.w1[...], self.patches[:, self.lanes(t)]), 0.0).astype(BF16)
+
+    def two(self, t):
+        bias = jnp.concatenate([self.b2[...]] * 2, axis=1)
+        self.h2[:, self.lanes(t)] = jnp.maximum(dot(self.w2[...], self.h1[:, self.lanes(t)]) + bias, 0.0).astype(BF16)
+
+    def three(self, t):
+        inside = jnp.concatenate([self.inside(j) for j in self.pair(t)], axis=1)
+        self.z[:, self.lanes(t)] = jnp.where(inside, dot(self.w3[...], self.h2[:, self.lanes(t)]), 0.0)
+
+    def z_block(self, tap, j):
+        if not self.first <= j < self.last:
+            return None
+        at = LANES * (j - self.first)
+        return self.z[self.outs * tap : self.outs * (tap + 1), at : at + LANES]
+
+    def out(self, j):
+        total = self.b3[...]
+        for dx in (0, -1, 1):
+            side = None
+            for dy in (-1, 0, 1):
+                part = moved(self.z_blocks[3 * (dy + 1) + dx + 1], j, self.width * dy + dx, self.lane)
+                side = part if side is None else side + part
+            total = total + (jnp.where(self.edge[dx], side, 0.0) if dx else side)
+        return total
 
 
 def gate(g):
     small = jnp.exp(-jnp.abs(g))
     sigmoid = jnp.where(g >= 0.0, 1.0, small) / (1.0 + small)
     return sigmoid, jnp.minimum(g, 0.0) - jnp.log(1.0 + small)
+
+
+STARTS = (0, 20, 40)
+
+
+def wavefront(tiles, lag, starts):
+    slots = []
+    for s, (n, start) in enumerate(zip(tiles, starts)):
+        for t in range(n):
+            for part, after in enumerate(lag):
+                slots.append((start + t + after, part, s, t))
+    return [(s, part, t) for _, part, s, t in sorted(slots, key=lambda x: (x[0], LATE[x[1]], x[2]))]
+
+
+LATE = (0, 1, 2, 3, 4, 5)
+ORDER = wavefront((5, 4, 4), (0, 1, 2, 3, 4, 5), STARTS)
 
 
 def kernel(
@@ -151,7 +241,9 @@
     loglik,
     pictures,
     packed,
+    packed_half,
     arrived,
+    own_rows,
     first2,
     second2,
     third2,
@@ -176,6 +268,8 @@
     sent_latent,
     got_latent,
     terms,
+    scratch_mid,
+    scratch_top,
     load_sem,
     small_sem,
     weight_sem,
@@ -197,8 +291,6 @@
         pltpu.make_async_copy(src, dst, small_sem.at[i])
         for i, (src, dst) in enumerate(zip(given2 + given3, small2 + small3))
     ]
-    for load in small_loads:
-        load.start()
     weight_loads = []
     for s in range(STEPS2):
         for src, dst in ((second_mid, second2), (first_mid, first2), (third_mid, third2)):
@@ -210,9 +302,6 @@
             weight_loads.append(
                 pltpu.make_async_copy(src.at[s], dst.at[s], weight_sem.at[len(weight_loads)])
             )
-    for load in weight_loads:
-        load.start()
-
     def in_image(d, body):
         if d == 0:
             body()
@@ -240,6 +329,8 @@
             in_image(far, greet_far)
 
     picture_load.wait()
+    for load in small_loads + weight_loads:
+        load.start()
     group = iota((8, LANES), 1) // COLS
     for i in range(8):
         tile = jnp.zeros((8, LANES), F32)
@@ -248,6 +339,7 @@
             part = jnp.concatenate([part, jnp.zeros((8, LANES - COLS), F32)], axis=1)
             tile = jnp.where(group == k, roll(part, COLS * k), tile)
         packed[i] = tile
+        packed_half[i] = tile.astype(BF16)
 
     def prepare_small():
         for load in small_loads:
@@ -304,9 +396,6 @@
         tall[217:, :] = jnp.zeros((KTOP - 217, HID), F32)
         w1_top[s] = tall[...].T.astype(BF16)
 
-    prepare_small()
-    prepare_mid(0)
-
     for edge in range(REACH + 1):
         blocks = REACH + 1 + edge
 
@@ -321,8 +410,8 @@
     def row_copy(d, k):
         to = (c + k) % CHAN
         return pltpu.make_async_remote_copy(
-            src_ref=packed.at[to],
-            dst_ref=arrived.at[8 * (REACH - d) + c],
+            src_ref=packed_half.at[to] if d else packed.at[to],
+            dst_ref=arrived.at[8 * (REACH - d) + c] if d else own_rows.at[c],
             send_sem=send_sem,
             recv_sem=recv_sem.at[REACH - d],
             device_id={"rows": r + d, "chan": to},
@@ -344,9 +433,10 @@
                 row_copy(d, k).start()
 
         sends(d, send)
-    arrived[8 * REACH + c] = packed[c]
-
-    for s in range(1, STEPS2):
+    own_rows[c] = packed[c]
+
+    prepare_small()
+    for s in range(STEPS2):
         prepare_mid(s)
     for s in range(STEPS3):
         prepare_top(s)
@@ -359,66 +449,98 @@
                 first += 2
             elif abs(d) == REACH:
                 last -= 2
-            elif d == 0:
-                last -= 1
-            tiles = arrived.at[pl.ds(first, last - first)]
+            tiles = arrived.at[pl.ds(first, last - first)] if d else own_rows.at[pl.ds(0, CHAN - 1)]
             pltpu.make_async_copy(tiles, tiles, recv_sem.at[d + REACH]).wait()
 
         in_image(d, receive)
 
-    rows_of_lanes = []
-    for k in range(3):
-        lanes_of_k = []
-        for g in range(WIDE // LANES):
+    lane128 = iota((1, LANES), 1)
+    for which in range(2):
+        spare = iota((16, WIDE), 0) == 0
+        scratch_mid[which][0][9 * 16 :, :] = jnp.where(spare, 1.0, 0.0).astype(BF16)
+
+    def inside_mid(j):
+        row = lane128 // COLS + 4 * j + 8 * (r - REACH)
+        return (row >= 0) & (row < 8 * ROWS)
+
+    def unpacked(g):
+        rows = []
+        for k in range(3):
             tile = None
             for j in range(4):
-                part = roll(arrived[4 * g + j], COLS * (j - k))
+                at = 4 * g + j
+                part = own_rows[at - 16] if 16 <= at < 24 else arrived[at].astype(F32)
+                part = turned(part, COLS * (k - j))
                 tile = part if tile is None else jnp.where(group == j, part, tile)
-            lanes_of_k.append(tile)
-        rows_of_lanes.append(jnp.concatenate(lanes_of_k, axis=1))
-    state = jnp.concatenate(rows_of_lanes + [ones_block(WIDE, 8, 0)], axis=0)
-
-    own = slice(NARROW // 2 - LANES, NARROW // 2 + LANES)
-    loglik_terms = jnp.zeros((16, 2 * LANES), F32)
+            rows.append(tile)
+        return jnp.concatenate(rows + [ones_block(LANES, 8, 0)], axis=0)
+
+    steps = []
     for s in range(STEPS2):
-        n = WIDE if s == 0 else NARROW
-        row = iota((1, n), 1) // COLS + (0 if s == 0 else 4) + 8 * (r - REACH)
-        inside = (row >= 0) & (row < 8 * ROWS)
-        u = split_mix(mix2[s], state)
-        q = jnp.where(inside, u[:16], 0.0)
-        out = conditioner(
-            q, inside, COLS, w1_mid.at[s], w2_mid.at[s], b2_mid.at[s], w3_mid.at[s], bias2[s]
+        first, last = (0, WIDE // LANES) if s == 0 else (1, WIDE // LANES - 1)
+        steps.append(
+            Step(
+                first, last, COLS, 12, inside_mid, mix2.at[s],
+                w1_mid.at[s], w2_mid.at[s], b2_mid.at[s], w3_mid.at[s], bias2.at[s], scratch_mid[s % 2],
+            )
         )
-        if s == 0:
-            u, out = u[:, LANES:-LANES], out[:, LANES:-LANES]
+    states = [{} for _ in range(STEPS2 + 1)]
+    own = (4, 5)
+    loglik_terms = []
+
+    def finish(s, j):
+        step = steps[s]
+        u, out = step.u[j], step.out(j)
         sigmoid, log_sigmoid = gate(out[:16])
-        loglik_terms += jnp.where(iota((16, 2 * LANES), 0) < 12, log_sigmoid[:, own], 0.0)
-        lower_half = iota((8, 1), 0) < 4
+        if j in own:
+            loglik_terms.append(log_sigmoid)
         mixed = (u[8:16] + out[8:16]) * pltpu.roll(sigmoid[8:16], 4, 0)
-        mixed = jnp.where(lower_half, u[8:16], mixed)
+        mixed = jnp.where(iota((8, 1), 0) < 4, u[8:16], mixed)
         rest = (u[16:24] + out[16:24]) * sigmoid[:8]
-        state = jnp.concatenate([u[:8], mixed, rest, ones_block(NARROW, 8, 0)], axis=0)
-
-    latent = state[:16, own]
-    loglik_terms -= jnp.where(iota((16, 2 * LANES), 0) < 12, 0.5 * latent * latent, 0.0)
+        states[s + 1][j] = jnp.concatenate([u[:8], mixed, rest, ones_block(LANES, 8, 0)], axis=0)
+
+    for s, part, t in ORDER:
+        step = steps[s]
+        if part == 0:
+            for j in step.pair(t):
+                if s == 0:
+                    states[0][j] = unpacked(j)
+            step.mix(t, lambda j: states[s][j])
+        elif part == 1:
+            step.patch(t)
+        elif part == 2:
+            step.one(t)
+        elif part == 3:
+            step.two(t)
+        elif part == 4:
+            step.three(t)
+        else:
+            for j in step.pair(t):
+                if s == STEPS2 - 1 or 1 <= j < WIDE // LANES - 1:
+                    finish(s, j)
+
+    final = states[STEPS2]
     for half in range(2):
-        sent_latent[half] = latent[:, LANES * half : LANES * (half + 1)]
-
-    kept = jnp.concatenate([state[16:24], state[8:16]], axis=0)
+        latent = final[own[half]][:16]
+        loglik_terms.append(-0.5 * latent * latent)
+        sent_latent[half] = latent
+    loglik_sum = jnp.where(iota((16, LANES), 0) < 12, sum(loglik_terms), 0.0)
+
     lane, to = iota((2 * LANES, 2 * LANES), 0), iota((2 * LANES, 2 * LANES), 1)
     p, col = lane // COLS, lane % COLS
     place = (2 * (p % 2) + col % 2) * 64 + (p // 2) * 16 + col // 2
     permutation = jnp.where(place == to, 1.0, 0.0).astype(BF16)
     streams = []
     for block in range(3):
-        rest = kept[:, LANES * (1 + 2 * block) : LANES * (3 + 2 * block)]
+        pair = [final[2 + 2 * block], final[3 + 2 * block]]
+        rest = jnp.concatenate([jnp.concatenate([x[16:24], x[8:16]], axis=0) for x in pair], axis=1)
         for _ in range(3):
             high = rest.astype(BF16)
             streams.append(high)
             rest = rest - high.astype(F32)
-    moved = dot(jnp.concatenate(streams, axis=0), permutation)
+    apart = dot(jnp.concatenate(streams, axis=0), permutation)
     blocks = [
-        moved[48 * b : 48 * b + 16] + moved[48 * b + 16 : 48 * b + 32] + moved[48 * b + 32 : 48 * b + 48]
+        apart[48 * b : 48 * b + 16] + apart[48 * b + 16 : 48 * b + 32] + apart[48 * b + 32 : 48 * b + 48]
         for b in range(3)
     ]
     lane64 = iota((16, LANES), 1) < 64
@@ -448,27 +570,37 @@
         latent_copy(k).start()
     got_latent[c] = sent_latent[c // 4]
 
-    row = iota((1, NTOP), 1) // 16
-    inside = (row + 4 * r >= 4) & (row + 4 * r < 4 * ROWS + 4) & (row < 12)
-    own_top = (iota((1, LANES), 1) >= 64)
+    def inside_top(j):
+        row = lane128 // 16 + 8 * j
+        return (row + 4 * r >= 4) & (row + 4 * r < 4 * ROWS + 4) & (row < 12)
+
+    own_top = lane128 >= 64
     top_terms = jnp.zeros((24, LANES), F32)
     for s in range(STEPS3):
-        u = split_mix(mix3[s], state)
-        q = jnp.where(inside, u[:24], 0.0)
-        out = conditioner(
-            q, inside, 16, w1_top.at[s], w2_top.at[s], b2_top.at[s], w3_top.at[s], bias3[s]
+        step = Step(
+            0, 2, 16, 24, inside_top, mix3.at[s],
+            w1_top.at[s], w2_top.at[s], b2_top.at[s], w3_top.at[s], bias3.at[s], scratch_top,
         )
-        sigmoid, log_sigmoid = gate(out[:24])
-        top_terms += log_sigmoid[:, :LANES]
-        rest = (u[24:] + out[24:]) * sigmoid
-        state = jnp.concatenate([u[:24], rest, ones_block(NTOP, 32, 0)], axis=0)
+        step.mix(0, lambda j: state[:, LANES * j : LANES * (j + 1)])
+        step.patch(0)
+        step.one(0)
+        step.two(0)
+        step.three(0)
+        blocks = []
+        for j in range(2 if s == 0 else 1):
+            u, out = step.u[j], step.out(j)
+            sigmoid, log_sigmoid = gate(out[:24])
+            if j == 0:
+                top_terms += log_sigmoid
+            blocks.append(jnp.concatenate([u[:24], (u[24:] + out[24:]) * sigmoid, ones_block(LANES, 32, 0)], axis=0))
+        state = jnp.concatenate(blocks, axis=1)
     z = state[:C3, :LANES]
     squares = z * z
     top_terms = jnp.where(own_top, top_terms - 0.5 * (squares[:24] + squares[24:]), 0.0)
 
     logdets = 256.0 * (jnp.sum(small2[1][...]) + jnp.sum(small2[4][...]))
     logdets += 64.0 * (jnp.sum(small3[1][...]) + jnp.sum(small3[4][...]))
-    total = jnp.sum(loglik_terms) + jnp.sum(top_terms) + logdets
+    total = jnp.sum(loglik_sum) + jnp.sum(top_terms) + logdets
     total = (total - 0.5 * LOG_TWO_PI * (12 * 256 + 48 * 64)) * (1.0 / DIMS)
     terms[r] = jnp.full((1, LANES), total, F32)
 
@@ -490,8 +622,8 @@
     others = got_latent.at[pl.ds(0, CHAN - 1)]
     pltpu.make_async_copy(others, others, latent_recv).wait()
     for i in range(8):
-        turned = pltpu.roll(got_latent[i], (LANES - COLS * (c % 4)) % LANES, 1)
-        latent_mid[i] = turned[:12, :COLS]
+        lined = pltpu.roll(got_latent[i], (LANES - COLS * (c % 4)) % LANES, 1)
+        latent_mid[12 * i : 12 * i + 12, :] = lined[:12, :COLS]
 
     others = terms.at[pl.ds(0, ROWS - 1)]
     pltpu.make_async_copy(others, others, term_recv).wait()
@@ -506,10 +638,23 @@
     for d in near:
 
         def left_here(d=d):
-            tiles = packed.at[pl.ds(0, CHAN - 1 if d == 0 else CHAN)]
+            tiles = packed_half if d else packed.at[pl.ds(0, CHAN - 1)]
             pltpu.make_async_copy(tiles, tiles, send_sem).wait()
 
         sends(d, left_here)
+
+
+def leave(latent_mid, latent_top, loglik, latent_mid_out, latent_top_out, loglik_out, sem):
+    copies = [
+        pltpu.make_async_copy(src, dst, sem.at[i])
+        for i, (src, dst) in enumerate(
+            ((latent_mid, latent_mid_out), (latent_top, latent_top_out), (loglik, loglik_out))
+        )
+    ]
+    for copy in copies:
+        copy.start()
+    for copy in copies:
+        copy.wait()
 
 
 def body(*given):
@@ -530,19 +675,29 @@
             pltpu.VMEM((steps, n), F32),
         )
 
+    def inner(taps, lanes, outs):
+        return (
+            pltpu.VMEM((taps, lanes), BF16),
+            pltpu.VMEM((HID, lanes), BF16),
+            pltpu.VMEM((HID, lanes), BF16),
+            pltpu.VMEM((9 * outs, lanes), F32),
+        )
+
     latent_mid, latent_top, loglik = pl.pallas_call(
         kernel,
         out_shape=(
-            jax.ShapeDtypeStruct((8, 12, COLS), F32),
-            jax.ShapeDtypeStruct((1, 4, 16, C3), F32),
-            jax.ShapeDtypeStruct((1, LANES), F32),
+            pltpu.VMEM((8 * 12, COLS), F32),
+            pltpu.VMEM((1, 4, 16, C3), F32),
+            pltpu.VMEM((1, LANES), F32),
         ),
         in_specs=[pl.BlockSpec(memory_space=pl.ANY)] * 23,
         out_specs=tuple(pl.BlockSpec(memory_space=pltpu.VMEM) for _ in range(3)),
         scratch_shapes=[
             pltpu.VMEM((8, C2, COLS), F32),
             pltpu.VMEM((8, 8, LANES), F32),
-            pltpu.VMEM((8 * BLOCKS, 8, LANES), F32),
+            pltpu.VMEM((8, 8, LANES), BF16),
+            pltpu.VMEM((8 * BLOCKS, 8, LANES), BF16),
+            pltpu.VMEM((8, 8, LANES), F32),
             pltpu.VMEM((STEPS2, 9, 12, HID), BF16),
             pltpu.VMEM((STEPS2, HID, HID), BF16),
             pltpu.VMEM((STEPS2, 9, C2, HID), BF16),
@@ -567,6 +722,8 @@
             pltpu.VMEM((2, 16, LANES), F32),
             pltpu.VMEM((CHAN, 16, LANES), F32),
             pltpu.VMEM((ROWS, 1, LANES), F32),
+            tuple(inner(KMID, WIDE, C2) for _ in range(2)),
+            inner(KTOP, NTOP, C3),
             pltpu.SemaphoreType.DMA,
             pltpu.SemaphoreType.DMA((16,)),
             pltpu.SemaphoreType.DMA((15,)),
@@ -579,6 +736,17 @@
         ],
         compiler_params=pltpu.CompilerParams(collective_id=0, has_side_effects=True, vmem_limit_bytes=60 * 2**20),
     )(*given)
+    latent_mid, latent_top, loglik = pl.pallas_call(
+        leave,
+        out_shape=(
+            jax.ShapeDtypeStruct((8 * 12, COLS), F32),
+            jax.ShapeDtypeStruct((1, 4, 16, C3), F32),
+            jax.ShapeDtypeStruct((1, LANES), F32),
+        ),
+        in_specs=[pl.BlockSpec(memory_space=pltpu.VMEM)] * 3,
+        out_specs=tuple(pl.BlockSpec(memory_space=pl.ANY) for _ in range(3)),
+        scratch_shapes=[pltpu.SemaphoreType.DMA((3,))],
+    )(*(pltpu.with_memory_space_constraint(x, pltpu.VMEM) for x in (latent_mid, latent_top, loglik)))
     return (
         latent_mid.reshape(8, 12, 1, COLS),
         latent_top.transpose(0, 3, 1, 2),

time: 46.2 us -> 35 us (0.76)
  Pallas kernels: 40.6 us -> 34.2 us
  local copies, waits for them, and re-layouts: 2.88 us -> 0 us
  between operations: 2.47 us -> 0.65 us
    pallas_call x1 -> x2, Pallas kernels: 40.6 us -> 34.2 us  [the longest x1 33.6 us: body(): pl.pallas_call(kernel, out_shape=(pltpu.VMEM((8 * 12, COLS), F32), pltpu....]
    unnamed x2 -> x0, local copies, waits for them, and re-layouts: 2.88 us -> none
where the time goes in v2:
time: 35 us; the launch traced here: 34.9 us
  Pallas kernels  34.2 us (98%)
  between operations  0.65 us (2%)
    pallas_call x1, Pallas kernels, body(): pl.pallas_call(kernel, out_shape=(pltpu.VMEM((8 * 12, COLS), F32), pltpu....  33.6 us

profile of v2, /device:TPU:1, one launch (start us, length us, event | category | flops | bytes accessed | tf_op | source)
XLA Modules:
  0.0 34.9 jit_solution(9953963733197792694)
XLA Ops:
  0.6 33.6 %shard_map.238 = (f32[96,32]{1,0:T(8,128)S(1)}, f32[1,4,16,48]{3,2,1,0:T(8,128)S(1)}, f32[1,128]{1,0:T(1,128)S(1)}) custom-call(f32[8,24,32]{2,1,0:T(8,128)} %bitcast.9, f32[3,24]{1,0:T(4,128)} %shift_mid.1, f32[3,24]{1,0:T(4,128)} %gain_mid.1, f32[3,24,24]{2,1,0:T(8,128)} %lower_mid.1, f32[3,24,24]{2,1,0:T(8,128)} %upper_mid.1, f32[3,24]{1,0:T(4,128)} %diag_mid.1, ...), custom_call_target="tpu_custom_call" | custom-call | tf_op jit(solution)/shard_map/pallas_call | solution.py:686
  34.2 0.7 %shard_map.239 = (f32[96,32]{1,0:T(8,128)}, f32[1,4,16,48]{3,2,1,0:T(8,128)}, f32[1,128]{1,0:T(1,128)}) custom-call(f32[96,32]{1,0:T(8,128)S(1)} %get-tuple-element.9.latent_mid, f32[1,4,16,48]{3,2,1,0:T(8,128)S(1)} %get-tuple-element.10.latent_top, f32[1,128]{1,0:T(1,128)S(1)} %get-tuple-element.11.loglik), custom_call_target="tpu_custom_call" | custom-call | tf_op jit(solution)/shard_map/pallas_call | solution.py:739

commit v3 on v2

--- a/solution.py
+++ b/solution.py
@@ -112,9 +112,15 @@
     return blocks
 
 
+def cut(rows, parts):
+    each = -(-rows // parts // 8) * 8
+    return [slice(at, min(at + each, rows)) for at in range(0, rows, each)]
+
+
 class Step:
-    def __init__(self, first, last, width, half, inside, mix, w1, w2, b2, w3, b3, scratch):
-        self.first, self.last, self.width, self.half = first, last, width, half
+    def __init__(self, first, last, width, half, inside, mix, w1, w2, b2, w3, b3, scratch, per=2, wrap=None, parts=1):
+        self.parts = parts
+        self.first, self.last, self.width, self.half, self.per, self.wrap = first, last, width, half, per, wrap
         self.inside, self.mix_w, self.w1, self.w2, self.b2, self.w3, self.b3 = inside, mix, w1, w2, b2, w3, b3
         self.patches, self.h1, self.h2, self.z = scratch
         self.outs = w3.shape[0] // 9
@@ -122,26 +128,26 @@
         self.lane = iota((1, LANES), 1)
         col = self.lane % width
         self.edge = {-1: col > 0, 1: col < width - 1}
-        self.q_blocks = cached(lambda j: self.q.get(j))
+        self.q_blocks = cached(lambda j: self.q.get(j % wrap if wrap else j))
         self.z_blocks = [
             cached(lambda j, t=t: self.z_block(t, j)) for t in range(9)
         ]
 
-    def tiles(self):
-        return (self.last - self.first) // 2
-
     def pair(self, t):
-        return self.first + 2 * t, self.first + 2 * t + 1
+        return [self.first + self.per * t + i for i in range(self.per)]
 
     def lanes(self, t):
-        return slice(2 * LANES * t, 2 * LANES * (t + 1))
+        return slice(self.per * LANES * t, self.per * LANES * (t + 1))
 
     def mix(self, t, state):
         pair = self.pair(t)
         u = split_mix(self.mix_w[...], jnp.concatenate([state(j) for j in pair], axis=1))
+        self.take(t, [u[:, LANES * i : LANES * (i + 1)] for i in range(self.per)])
+
+    def take(self, t, u):
         rows = 16 if self.half == 12 else 24
-        for i, j in enumerate(pair):
-            self.u[j] = u[:, LANES * i : LANES * (i + 1)]
+        for i, j in enumerate(self.pair(t)):
+            self.u[j] = u[i]
             self.q[j] = jnp.where(self.inside(j), self.u[j][:rows], 0.0)
             if rows == 16:
                 self.q[j] = self.q[j].astype(BF16)
@@ -159,21 +165,29 @@
             for i, tap in enumerate(taps):
                 self.patches[16 * i : 16 * (i + 1), self.lanes(t)] = tap
         else:
-            taps.append(ones_block(2 * LANES, 8, 0))
+            taps.append(ones_block(self.per * LANES, 8, 0))
             self.patches[:, self.lanes(t)] = jnp.concatenate(taps, axis=0).astype(BF16)
 
     def one(self, t):
-        self.h1[:, self.lanes(t)] = jnp.maximum(dot(self.w1[...], self.patches[:, self.lanes(t)]), 0.0).astype(BF16)
+        patches = self.patches[:, self.lanes(t)]
+        for m in cut(HID, self.parts):
+            self.h1[m, self.lanes(t)] = jnp.maximum(dot(self.w1[m, :], patches), 0.0).astype(BF16)
 
     def two(self, t):
-        bias = jnp.concatenate([self.b2[...]] * 2, axis=1)
-        self.h2[:, self.lanes(t)] = jnp.maximum(dot(self.w2[...], self.h1[:, self.lanes(t)]) + bias, 0.0).astype(BF16)
+        h1 = self.h1[:, self.lanes(t)]
+        for m in cut(HID, self.parts):
+            bias = jnp.concatenate([self.b2[m, :]] * self.per, axis=1)
+            self.h2[m, self.lanes(t)] = jnp.maximum(dot(self.w2[m, :], h1) + bias, 0.0).astype(BF16)
 
     def three(self, t):
         inside = jnp.concatenate([self.inside(j) for j in self.pair(t)], axis=1)
-        self.z[:, self.lanes(t)] = jnp.where(inside, dot(self.w3[...], self.h2[:, self.lanes(t)]), 0.0)
+        h2 = self.h2[:, self.lanes(t)]
+        for m in cut(9 * self.outs, self.parts):
+            self.z[m, self.lanes(t)] = jnp.where(inside, dot(self.w3[m, :], h2), 0.0)
 
     def z_block(self, tap, j):
+        if self.wrap:
+            j = j % self.wrap
         if not self.first <= j < self.last:
             return None
         at = LANES * (j - self.first)
@@ -196,20 +210,33 @@
     return sigmoid, jnp.minimum(g, 0.0) - jnp.log(1.0 + small)
 
 
-STARTS = (0, 20, 40)
-
-
-def wavefront(tiles, lag, starts):
-    slots = []
-    for s, (n, start) in enumerate(zip(tiles, starts)):
-        for t in range(n):
-            for part, after in enumerate(lag):
-                slots.append((start + t + after, part, s, t))
-    return [(s, part, t) for _, part, s, t in sorted(slots, key=lambda x: (x[0], LATE[x[1]], x[2]))]
-
-
-LATE = (0, 1, 2, 3, 4, 5)
-ORDER = wavefront((5, 4, 4), (0, 1, 2, 3, 4, 5), STARTS)
+def emission(orders, firsts, gaps):
+    slots, done = [], {}
+    for s, (order, first) in enumerate(zip(orders, firsts)):
+        start = gaps[s]
+        near = lambda t: [x for x in (t - 1, t, t + 1) if x in order]
+        at = {}
+        for i, t in enumerate(order):
+            need = [done[j] for j in (first + 2 * t, first + 2 * t + 1)] if s else []
+            at[0, t] = max([start + i] + need)
+        last = 0
+        for t in order:
+            at[1, t] = max(at[0, x] for x in near(t)) + 1
+            at[2, t] = last = max(at[1, t], last + 1)
+            at[3, t] = at[2, t] + LAG
+            at[4, t] = at[2, t] + 2 * LAG
+        for t in order:
+            at[5, t] = max(at[4, x] for x in near(t)) + 1
+            for j in (first + 2 * t, first + 2 * t + 1):
+                done[j] = at[5, t]
+        slots += [(slot, part, order.index(t), s, t) for (part, t), slot in at.items()]
+    return [(s, part, t) for _, part, _, s, t in sorted(slots, key=lambda x: (x[0], x[3], x[1], x[2]))]
+
+
+LAG = 1
+MID_PARTS = 2
+TOP_PARTS = 4
+ORDER = emission(((0, 1, 2, 3, 4), (0, 1, 2, 3), (0, 1, 2, 3)), (0, 1, 1), (0, 0, 0))
 
 
 def kernel(
@@ -291,6 +318,8 @@
         pltpu.make_async_copy(src, dst, small_sem.at[i])
         for i, (src, dst) in enumerate(zip(given2 + given3, small2 + small3))
     ]
+    for load in small_loads:
+        load.start()
     weight_loads = []
     for s in range(STEPS2):
         for src, dst in ((second_mid, second2), (first_mid, first2), (third_mid, third2)):
@@ -311,52 +340,41 @@
     near = range(-REACH, REACH + 1)
 
     arrived[...] = jnp.zeros_like(arrived)
-    for d in near:
-
-        def greet(d=d):
-            for k in range(1 if d == 0 else 0, CHAN):
-                pl.semaphore_signal(
-                    barrier, 1, device_id={"rows": r + d, "chan": (c + k) % CHAN}, device_id_type=MESH
-                )
-
-        in_image(d, greet)
-    for d in range(REACH + 1, ROWS):
-        for far in (-d, d):
-
-            def greet_far(far=far):
-                pl.semaphore_signal(barrier, 1, device_id={"rows": r + far}, device_id_type=MESH)
-
-            in_image(far, greet_far)
+    def greet(d):
+        for to in range(CHAN):
+
+            def signal(to=to):
+                pl.semaphore_signal(barrier, 1, device_id={"rows": r + d, "chan": to}, device_id_type=MESH)
+
+            if d == 0:
+                pl.when(c != to)(signal)
+            else:
+                signal()
+
+    def greet_far(d):
+        pl.semaphore_signal(barrier, 1, device_id={"rows": r + d}, device_id_type=MESH)
+
+    for d in sorted(range(1 - ROWS, ROWS), key=lambda d: (abs(d) > REACH, -abs(d))):
+        in_image(d, lambda d=d: greet(d) if abs(d) <= REACH else greet_far(d))
 
     picture_load.wait()
-    for load in small_loads + weight_loads:
-        load.start()
-    group = iota((8, LANES), 1) // COLS
-    for i in range(8):
-        tile = jnp.zeros((8, LANES), F32)
-        for k in range(3):
-            part = pictures[i, 8 * k : 8 * k + 8, :]
-            part = jnp.concatenate([part, jnp.zeros((8, LANES - COLS), F32)], axis=1)
-            tile = jnp.where(group == k, roll(part, COLS * k), tile)
-        packed[i] = tile
-        packed_half[i] = tile.astype(BF16)
+    def prepare_mix(s):
+        shift, gain, lower, upper, diag, _, second_b, third_b = small2
+        a, b = mixing(shift[s : s + 1], gain[s : s + 1], lower[s], upper[s], diag[s : s + 1])
+        to_rows = jnp.where(place_mid(C2, 0) == iota((C2, C2), 1), 1.0, 0.0)
+        a, b = exact_dot(to_rows, a), exact_dot(to_rows, b)
+        if s:
+            to_columns = jnp.where(place_mid(C2, 1) == iota((C2, C2), 0), 1.0, 0.0)
+            a = exact_dot(a, to_columns)
+        mix2[s] = stacked(a, b, 32, C2)
+        extra = third_b[s : s + 1] + jnp.where(iota((1, C2), 1) < C2 // 2, 2.0, 0.0)
+        bias2[s] = jnp.sum(to_rows * extra, axis=1, keepdims=True)
 
     def prepare_small():
-        for load in small_loads:
-            load.wait()
-        shift, gain, lower, upper, diag, _, second_b, third_b = small2
         for s in range(STEPS2):
-            a, b = mixing(shift[s : s + 1], gain[s : s + 1], lower[s], upper[s], diag[s : s + 1])
-            to_rows = jnp.where(place_mid(C2, 0) == iota((C2, C2), 1), 1.0, 0.0)
-            a = exact_dot(to_rows, a)
             if s:
-                to_columns = jnp.where(place_mid(C2, 1) == iota((C2, C2), 0), 1.0, 0.0)
-                a = exact_dot(a, to_columns)
-            b = exact_dot(to_rows, b)
-            mix2[s] = stacked(a, b, 32, C2)
-            extra = third_b[s : s + 1] + jnp.where(iota((1, C2), 1) < C2 // 2, 2.0, 0.0)
-            bias2[s] = jnp.sum(to_rows * extra, axis=1, keepdims=True)
-            b2_mid[s] = jnp.broadcast_to(second_b[s : s + 1], (LANES, HID)).T
+                prepare_mix(s)
+            b2_mid[s] = jnp.broadcast_to(small2[6][s : s + 1], (LANES, HID)).T
         shift, gain, lower, upper, diag, _, second_b, third_b = small3
         for s in range(STEPS3):
             a, b = mixing(shift[s : s + 1], gain[s : s + 1], lower[s], upper[s], diag[s : s + 1])
@@ -396,6 +414,34 @@
         tall[217:, :] = jnp.zeros((KTOP - 217, HID), F32)
         w1_top[s] = tall[...].T.astype(BF16)
 
+    for load in small_loads:
+        load.wait()
+    for load in weight_loads:
+        load.start()
+    prepare_mix(0)
+    group = iota((8, LANES), 1) // COLS
+    pictures_in = []
+    for half in range(2):
+        rows = []
+        for k in range(3):
+            tile = None
+            for j in range(4):
+                part = pictures[4 * half + j, 8 * k : 8 * k + 8, :]
+                part = jnp.concatenate([part, jnp.zeros((8, LANES - COLS), F32)], axis=1)
+                part = turned(part, -COLS * j)
+                tile = part if tile is None else jnp.where(group == j, part, tile)
+            rows.append(tile)
+        pictures_in.append(jnp.concatenate(rows + [ones_block(LANES, 8, 0)], axis=0))
+    mixed_in = split_mix(mix2[0], jnp.concatenate(pictures_in, axis=1))
+
+    for i in range(8):
+        tile = jnp.zeros((8, LANES), F32)
+        for k in range(3):
+            part = mixed_in[8 * k : 8 * k + 8, LANES * (i // 4) : LANES * (i // 4 + 1)]
+            tile = jnp.where(group == k, turned(part, COLS * (i % 4 - k)), tile)
+        packed[i] = tile
+        packed_half[i] = tile.astype(BF16)
+
     for edge in range(REACH + 1):
         blocks = REACH + 1 + edge
 
@@ -408,7 +454,7 @@
             pl.when((r >= edge) & (r <= ROWS - 1 - edge))(meet)
 
     def row_copy(d, k):
-        to = (c + k) % CHAN
+        to = lax.rem(c + k, CHAN)
         return pltpu.make_async_remote_copy(
             src_ref=packed_half.at[to] if d else packed.at[to],
             dst_ref=arrived.at[8 * (REACH - d) + c] if d else own_rows.at[c],
@@ -429,7 +475,7 @@
     for d in sorted(near, key=lambda d: -abs(d)):
 
         def send(d=d):
-            for k in range(1 if d == 0 else 0, CHAN):
+            for k in (4, 3, 5, 2, 6, 1, 7) + (() if d == 0 else (0,)):
                 row_copy(d, k).start()
 
         sends(d, send)
@@ -441,18 +487,21 @@
     for s in range(STEPS3):
         prepare_top(s)
 
+    def arrive(d):
+        first, last = 8 * (d + REACH), 8 * (d + REACH) + 8
+        if d == -REACH:
+            first += 2
+        elif d == REACH:
+            last -= 2
+        tiles = arrived.at[pl.ds(first, last - first)] if d else own_rows.at[pl.ds(0, CHAN - 1)]
+
+        def wait():
+            pltpu.make_async_copy(tiles, tiles, recv_sem.at[d + REACH]).wait()
+
+        in_image(d, wait)
+
     for d in near:
-
-        def receive(d=d):
-            first, last = 8 * (d + REACH), 8 * (d + REACH) + 8
-            if d == -REACH:
-                first += 2
-            elif abs(d) == REACH:
-                last -= 2
-            tiles = arrived.at[pl.ds(first, last - first)] if d else own_rows.at[pl.ds(0, CHAN - 1)]
-            pltpu.make_async_copy(tiles, tiles, recv_sem.at[d + REACH]).wait()
-
-        in_image(d, receive)
+        arrive(d)
 
     lane128 = iota((1, LANES), 1)
     for which in range(2):
@@ -473,7 +522,7 @@
                 part = turned(part, COLS * (k - j))
                 tile = part if tile is None else jnp.where(group == j, part, tile)
             rows.append(tile)
-        return jnp.concatenate(rows + [ones_block(LANES, 8, 0)], axis=0)
+        return jnp.concatenate(rows, axis=0)
 
     steps = []
     for s in range(STEPS2):
@@ -481,7 +530,7 @@
         steps.append(
             Step(
                 first, last, COLS, 12, inside_mid, mix2.at[s],
-                w1_mid.at[s], w2_mid.at[s], b2_mid.at[s], w3_mid.at[s], bias2.at[s], scratch_mid[s % 2],
+                w1_mid.at[s], w2_mid.at[s], b2_mid.at[s], w3_mid.at[s], bias2.at[s], scratch_mid[s % 2], parts=MID_PARTS,
             )
         )
     states = [{} for _ in range(STEPS2 + 1)]
@@ -502,10 +551,10 @@
     for s, part, t in ORDER:
         step = steps[s]
         if part == 0:
-            for j in step.pair(t):
-                if s == 0:
-                    states[0][j] = unpacked(j)
-            step.mix(t, lambda j: states[s][j])
+            if s == 0:
+                step.take(t, [unpacked(j) for j in step.pair(t)])
+            else:
+                step.mix(t, lambda j: states[s][j])
         elif part == 1:
             step.patch(t)
         elif part == 2:
@@ -534,29 +583,27 @@
     for block in range(3):
         pair = [final[2 + 2 * block], final[3 + 2 * block]]
         rest = jnp.concatenate([jnp.concatenate([x[16:24], x[8:16]], axis=0) for x in pair], axis=1)
-        for _ in range(3):
+        for _ in range(2):
             high = rest.astype(BF16)
             streams.append(high)
             rest = rest - high.astype(F32)
     apart = dot(jnp.concatenate(streams, axis=0), permutation)
     blocks = [
-        apart[48 * b : 48 * b + 16] + apart[48 * b + 16 : 48 * b + 32] + apart[48 * b + 32 : 48 * b + 48]
+        apart[32 * b : 32 * b + 16] + apart[32 * b + 16 : 32 * b + 32]
         for b in range(3)
     ]
-    lane64 = iota((16, LANES), 1) < 64
     squeezed = []
     for ij in range(4):
-        half = LANES * (ij // 2)
-        at = [b[:, half : half + LANES] for b in blocks]
-        if ij % 2 == 0:
-            left, right = jnp.where(lane64, at[0], roll(at[1], 64)), at[2]
-        else:
-            left, right = jnp.where(lane64, roll(at[0], 64), at[1]), roll(at[2], 64)
+        half, sub = LANES * (ij // 2), 64 * (ij % 2)
+        rows0, rows4, rows8 = (b[:, half : half + LANES] for b in blocks)
+        left = jnp.where(lane128 < 32, turned(rows0, sub + 32), turned(rows4, sub - 32))
+        left = jnp.where(lane128 < 96, left, turned(rows8, sub - 96))
+        right = jnp.where(lane128 < 96, turned(rows8, sub + 32), turned(rows0, sub - 96))
         squeezed.append(jnp.concatenate([left, right], axis=1))
     state = jnp.concatenate(squeezed + [ones_block(NTOP, 16, 0)], axis=0)
 
     def latent_copy(k):
-        to = (c + k) % CHAN
+        to = lax.rem(c + k, CHAN)
         return pltpu.make_async_remote_copy(
             src_ref=sent_latent.at[to // 4],
             dst_ref=got_latent.at[c],
@@ -571,29 +618,26 @@
     got_latent[c] = sent_latent[c // 4]
 
     def inside_top(j):
-        row = lane128 // 16 + 8 * j
+        row = (lane128 // 16 + 8 * j + 2) % 16
         return (row + 4 * r >= 4) & (row + 4 * r < 4 * ROWS + 4) & (row < 12)
 
-    own_top = lane128 >= 64
+    own_top = (lane128 >= 32) & (lane128 < 96)
     top_terms = jnp.zeros((24, LANES), F32)
     for s in range(STEPS3):
         step = Step(
-            0, 2, 16, 24, inside_top, mix3.at[s],
+            0, 2 - s, 16, 24, inside_top, mix3.at[s],
             w1_top.at[s], w2_top.at[s], b2_top.at[s], w3_top.at[s], bias3.at[s], scratch_top,
+            per=2 - s, wrap=None if s else 2, parts=TOP_PARTS,
         )
         step.mix(0, lambda j: state[:, LANES * j : LANES * (j + 1)])
         step.patch(0)
         step.one(0)
         step.two(0)
         step.three(0)
-        blocks = []
-        for j in range(2 if s == 0 else 1):
-            u, out = step.u[j], step.out(j)
-            sigmoid, log_sigmoid = gate(out[:24])
-            if j == 0:
-                top_terms += log_sigmoid
-            blocks.append(jnp.concatenate([u[:24], (u[24:] + out[24:]) * sigmoid, ones_block(LANES, 32, 0)], axis=0))
-        state = jnp.concatenate(blocks, axis=1)
+        u, out = step.u[0], step.out(0)
+        sigmoid, log_sigmoid = gate(out[:24])
+        top_terms += log_sigmoid
+        state = jnp.concatenate([u[:24], (u[24:] + out[24:]) * sigmoid, ones_block(LANES, 32, 0)], axis=0)
     z = state[:C3, :LANES]
     squares = z * z
     top_terms = jnp.where(own_top, top_terms - 0.5 * (squares[:24] + squares[24:]), 0.0)
@@ -614,10 +658,10 @@
             device_id_type=MESH,
         )
 
-    for k in range(1, ROWS):
+    for k in (4, 3, 5, 2, 6, 1, 7):
         term_copy(k).start()
 
-    latent_top[0] = z.T[64:].reshape(4, 16, C3)
+    latent_top[0] = z.T[32:96].reshape(4, 16, C3)
 
     others = got_latent.at[pl.ds(0, CHAN - 1)]
     pltpu.make_async_copy(others, others, latent_recv).wait()

time: 35 us -> 34.1 us (0.974)
  Pallas kernels: 34.2 us -> 33.3 us
    pallas_call x1, Pallas kernels: 33.6 us -> 32.6 us  [body(): pl.pallas_call(kernel, out_shape=(pltpu.VMEM((8 * 12, COLS), F32), pltpu....]
where the time goes in v3:
time: 34.1 us; the launch traced here: 34 us
  Pallas kernels  33.3 us (98%)
  between operations  0.65 us (2%)
    pallas_call x1, Pallas kernels, body(): pl.pallas_call(kernel, out_shape=(pltpu.VMEM((8 * 12, COLS), F32), pltpu....  32.6 us

profile of v3, /device:TPU:1, one launch (start us, length us, event | category | flops | bytes accessed | tf_op | source)
XLA Modules:
  0.0 34.0 jit_solution(5231804222783775497)
XLA Ops:
  0.6 32.6 %shard_map.238 = (f32[96,32]{1,0:T(8,128)S(1)}, f32[1,4,16,48]{3,2,1,0:T(8,128)S(1)}, f32[1,128]{1,0:T(1,128)S(1)}) custom-call(f32[8,24,32]{2,1,0:T(8,128)} %bitcast.9, f32[3,24]{1,0:T(4,128)} %shift_mid.1, f32[3,24]{1,0:T(4,128)} %gain_mid.1, f32[3,24,24]{2,1,0:T(8,128)} %lower_mid.1, f32[3,24,24]{2,1,0:T(8,128)} %upper_mid.1, f32[3,24]{1,0:T(4,128)} %diag_mid.1, ...), custom_call_target="tpu_custom_call" | custom-call | tf_op jit(solution)/shard_map/pallas_call | solution.py:730
  33.3 0.7 %shard_map.239 = (f32[96,32]{1,0:T(8,128)}, f32[1,4,16,48]{3,2,1,0:T(8,128)}, f32[1,128]{1,0:T(1,128)}) custom-call(f32[96,32]{1,0:T(8,128)S(1)} %get-tuple-element.9.latent_mid, f32[1,4,16,48]{3,2,1,0:T(8,128)S(1)} %get-tuple-element.10.latent_top, f32[1,128]{1,0:T(1,128)S(1)} %get-tuple-element.11.loglik), custom_call_target="tpu_custom_call" | custom-call | tf_op jit(solution)/shard_map/pallas_call | solution.py:783

commit v4 on v3

--- a/solution.py
+++ b/solution.py
@@ -139,18 +139,29 @@
     def lanes(self, t):
         return slice(self.per * LANES * t, self.per * LANES * (t + 1))
 
-    def mix(self, t, state):
-        pair = self.pair(t)
-        u = split_mix(self.mix_w[...], jnp.concatenate([state(j) for j in pair], axis=1))
-        self.take(t, [u[:, LANES * i : LANES * (i + 1)] for i in range(self.per)])
-
-    def take(self, t, u):
+    def mix(self, blocks, state):
+        if len(self.mix_w.shape) == 3:
+            n = self.mix_w.shape[0] - 1
+            x = [state(j) for j in blocks]
+            sums = [[self.mix_w[n]] * len(x), [None] * len(x)]
+            for k in range(n):
+                weights = self.mix_w[k]
+                for i, y in enumerate(x):
+                    term, so_far = weights * y[k : k + 1, :], sums[k % 2][i]
+                    sums[k % 2][i] = term if so_far is None else so_far + term
+            for i, j in enumerate(blocks):
+                self.take(j, sums[0][i] + sums[1][i])
+            return
+        u = split_mix(self.mix_w[...], jnp.concatenate([state(j) for j in blocks], axis=1))
+        for i, j in enumerate(blocks):
+            self.take(j, u[:, LANES * i : LANES * (i + 1)])
+
+    def take(self, j, u):
         rows = 16 if self.half == 12 else 24
-        for i, j in enumerate(self.pair(t)):
-            self.u[j] = u[i]
-            self.q[j] = jnp.where(self.inside(j), self.u[j][:rows], 0.0)
-            if rows == 16:
-                self.q[j] = self.q[j].astype(BF16)
+        self.u[j] = u
+        self.q[j] = jnp.where(self.inside(j), u[:rows], 0.0)
+        if rows == 16:
+            self.q[j] = self.q[j].astype(BF16)
 
     def patch(self, t):
         taps = []
@@ -210,33 +221,31 @@
     return sigmoid, jnp.minimum(g, 0.0) - jnp.log(1.0 + small)
 
 
-def emission(orders, firsts, gaps):
+def emission(windows):
     slots, done = [], {}
-    for s, (order, first) in enumerate(zip(orders, firsts)):
-        start = gaps[s]
-        near = lambda t: [x for x in (t - 1, t, t + 1) if x in order]
+    for s, (first, last) in enumerate(windows):
+        blocks, tiles = range(first, last), range((last - first) // 2)
         at = {}
-        for i, t in enumerate(order):
-            need = [done[j] for j in (first + 2 * t, first + 2 * t + 1)] if s else []
-            at[0, t] = max([start + i] + need)
-        last = 0
-        for t in order:
-            at[1, t] = max(at[0, x] for x in near(t)) + 1
-            at[2, t] = last = max(at[1, t], last + 1)
+        for j in blocks:
+            at[0, j] = done[j] if s else (j - first) // 2
+        end = -1
+        for t in tiles:
+            seen = [j for j in range(first + 2 * t - 1, first + 2 * t + 3) if j in blocks]
+            at[1, t] = max(at[0, j] for j in seen) + 1
+            at[2, t] = end = max(at[1, t], end + 1)
             at[3, t] = at[2, t] + LAG
             at[4, t] = at[2, t] + 2 * LAG
-        for t in order:
-            at[5, t] = max(at[4, x] for x in near(t)) + 1
-            for j in (first + 2 * t, first + 2 * t + 1):
-                done[j] = at[5, t]
-        slots += [(slot, part, order.index(t), s, t) for (part, t), slot in at.items()]
-    return [(s, part, t) for _, part, _, s, t in sorted(slots, key=lambda x: (x[0], x[3], x[1], x[2]))]
+        for j in blocks:
+            at[5, j] = max(at[4, (x - first) // 2] for x in (j - 1, j, j + 1) if x in blocks) + 1
+            done[j] = at[5, j]
+        slots += [(slot, s, part, x) for (part, x), slot in at.items()]
+    return [(s, part, x) for _, s, part, x in sorted(slots)]
 
 
 LAG = 1
 MID_PARTS = 2
 TOP_PARTS = 4
-ORDER = emission(((0, 1, 2, 3, 4), (0, 1, 2, 3), (0, 1, 2, 3)), (0, 1, 1), (0, 0, 0))
+ORDER = emission(((0, 10), (1, 9), (1, 9)))
 
 
 def kernel(
@@ -280,7 +289,9 @@
     small2,
     small3,
     mix2,
+    wide2,
     mix3,
+    wide3,
     bias2,
     bias3,
     tall,
@@ -295,6 +306,7 @@
     sent_latent,
     got_latent,
     terms,
+    base,
     scratch_mid,
     scratch_top,
     load_sem,
@@ -366,7 +378,12 @@
         if s:
             to_columns = jnp.where(place_mid(C2, 1) == iota((C2, C2), 0), 1.0, 0.0)
             a = exact_dot(a, to_columns)
-        mix2[s] = stacked(a, b, 32, C2)
+        if s == 0:
+            mix2[...] = stacked(a, b, 32, C2)
+        else:
+            for k in range(C2):
+                wide2[s - 1, k] = jnp.broadcast_to(a[:, k : k + 1], (C2, LANES))
+            wide2[s - 1, C2] = jnp.broadcast_to(b, (C2, LANES))
         extra = third_b[s : s + 1] + jnp.where(iota((1, C2), 1) < C2 // 2, 2.0, 0.0)
         bias2[s] = jnp.sum(to_rows * extra, axis=1, keepdims=True)
 
@@ -383,12 +400,20 @@
                 row = n // 4
                 at = (n % 4) * 16 + jnp.where(row < 8, row, row + 4)
                 a = exact_dot(a, jnp.where(at == k, 1.0, 0.0))
-                mix3[s] = stacked(a, b, 80, 64)
+                mix3[...] = stacked(a, b, 80, 64)
             else:
-                mix3[s] = stacked(a, b, 80, C3)
+                for k in range(C3):
+                    wide3[k] = jnp.broadcast_to(a[:, k : k + 1], (C3, LANES))
+                wide3[C3] = jnp.broadcast_to(b, (C3, LANES))
             extra = third_b[s : s + 1] + jnp.where(iota((1, C3), 1) < C3 // 2, 2.0, 0.0)
             bias3[s] = column(extra)
             b2_top[s] = jnp.broadcast_to(second_b[s : s + 1], (LANES, HID)).T
+
+        logdets = 256.0 * (jnp.sum(small2[1][...]) + jnp.sum(small2[4][...]))
+        logdets += 64.0 * (jnp.sum(small3[1][...]) + jnp.sum(small3[4][...]))
+        logdets -= 0.5 * LOG_TWO_PI * (12 * 256 + 48 * 64)
+        corner = (iota((8, LANES), 0) == 0) & (iota((8, LANES), 1) == 0)
+        base[...] = jnp.where(corner, logdets, 0.0)
 
     def prepare_mid(s):
         for i in range(3):
@@ -432,7 +457,7 @@
                 tile = part if tile is None else jnp.where(group == j, part, tile)
             rows.append(tile)
         pictures_in.append(jnp.concatenate(rows + [ones_block(LANES, 8, 0)], axis=0))
-    mixed_in = split_mix(mix2[0], jnp.concatenate(pictures_in, axis=1))
+    mixed_in = split_mix(mix2[...], jnp.concatenate(pictures_in, axis=1))
 
     for i in range(8):
         tile = jnp.zeros((8, LANES), F32)
@@ -529,7 +554,7 @@
         first, last = (0, WIDE // LANES) if s == 0 else (1, WIDE // LANES - 1)
         steps.append(
             Step(
-                first, last, COLS, 12, inside_mid, mix2.at[s],
+                first, last, COLS, 12, inside_mid, wide2.at[max(s - 1, 0)],
                 w1_mid.at[s], w2_mid.at[s], b2_mid.at[s], w3_mid.at[s], bias2.at[s], scratch_mid[s % 2], parts=MID_PARTS,
             )
         )
@@ -546,27 +571,25 @@
         mixed = (u[8:16] + out[8:16]) * pltpu.roll(sigmoid[8:16], 4, 0)
         mixed = jnp.where(iota((8, 1), 0) < 4, u[8:16], mixed)
         rest = (u[16:24] + out[16:24]) * sigmoid[:8]
-        states[s + 1][j] = jnp.concatenate([u[:8], mixed, rest, ones_block(LANES, 8, 0)], axis=0)
-
-    for s, part, t in ORDER:
+        states[s + 1][j] = jnp.concatenate([u[:8], mixed, rest], axis=0)
+
+    for s, part, at in ORDER:
         step = steps[s]
         if part == 0:
             if s == 0:
-                step.take(t, [unpacked(j) for j in step.pair(t)])
+                step.take(at, unpacked(at))
             else:
-                step.mix(t, lambda j: states[s][j])
+                step.mix([at], lambda j: states[s][j])
         elif part == 1:
-            step.patch(t)
+            step.patch(at)
         elif part == 2:
-            step.one(t)
+            step.one(at)
         elif part == 3:
-            step.two(t)
+            step.two(at)
         elif part == 4:
-            step.three(t)
-        else:
-            for j in step.pair(t):
-                if s == STEPS2 - 1 or 1 <= j < WIDE // LANES - 1:
-                    finish(s, j)
+            step.three(at)
+        elif s == STEPS2 - 1 or 1 <= at < WIDE // LANES - 1:
+            finish(s, at)
 
     final = states[STEPS2]
     for half in range(2):
@@ -625,11 +648,11 @@
     top_terms = jnp.zeros((24, LANES), F32)
     for s in range(STEPS3):
         step = Step(
-            0, 2 - s, 16, 24, inside_top, mix3.at[s],
+            0, 2 - s, 16, 24, inside_top, wide3 if s else mix3,
             w1_top.at[s], w2_top.at[s], b2_top.at[s], w3_top.at[s], bias3.at[s], scratch_top,
             per=2 - s, wrap=None if s else 2, parts=TOP_PARTS,
         )
-        step.mix(0, lambda j: state[:, LANES * j : LANES * (j + 1)])
+        step.mix(range(2 - s), lambda j: state[:, LANES * j : LANES * (j + 1)])
         step.patch(0)
         step.one(0)
         step.two(0)
@@ -637,16 +660,14 @@
         u, out = step.u[0], step.out(0)
         sigmoid, log_sigmoid = gate(out[:24])
         top_terms += log_sigmoid
-        state = jnp.concatenate([u[:24], (u[24:] + out[24:]) * sigmoid, ones_block(LANES, 32, 0)], axis=0)
-    z = state[:C3, :LANES]
+        state = jnp.concatenate([u[:24], (u[24:] + out[24:]) * sigmoid], axis=0)
+    z = state
     squares = z * z
     top_terms = jnp.where(own_top, top_terms - 0.5 * (squares[:24] + squares[24:]), 0.0)
 
-    logdets = 256.0 * (jnp.sum(small2[1][...]) + jnp.sum(small2[4][...]))
-    logdets += 64.0 * (jnp.sum(small3[1][...]) + jnp.sum(small3[4][...]))
-    total = jnp.sum(loglik_sum) + jnp.sum(top_terms) + logdets
-    total = (total - 0.5 * LOG_TWO_PI * (12 * 256 + 48 * 64)) * (1.0 / DIMS)
-    terms[r] = jnp.full((1, LANES), total, F32)
+    last = top_terms[:8] + top_terms[8:16] + top_terms[16:]
+    last += loglik_sum[:8] + loglik_sum[8:] + base[...]
+    terms[r] = jnp.sum(last, axis=0, keepdims=True) * (1.0 / DIMS)
 
     def term_copy(k):
         return pltpu.make_async_remote_copy(
@@ -674,7 +695,7 @@
     whole = terms[0]
     for i in range(1, ROWS):
         whole = whole + terms[i]
-    loglik[...] = whole
+    loglik[...] = jnp.broadcast_to(jnp.sum(whole, axis=1, keepdims=True), (1, LANES))
 
     pltpu.make_async_copy(others, others, term_send).wait()
     others = got_latent.at[pl.ds(0, CHAN - 1)]
@@ -750,8 +771,10 @@
             pltpu.VMEM((STEPS3, 9, C3, HID), BF16),
             small(C2, STEPS2),
             small(C3, STEPS3),
-            pltpu.VMEM((STEPS2, C2, 96), BF16),
-            pltpu.VMEM((STEPS3, C3, 240), BF16),
+            pltpu.VMEM((C2, 96), BF16),
+            pltpu.VMEM((STEPS2 - 1, C2 + 1, C2, LANES), F32),
+            pltpu.VMEM((C3, 240), BF16),
+            pltpu.VMEM((C3 + 1, C3, LANES), F32),
             pltpu.VMEM((STEPS2, C2, 1), F32),
             pltpu.VMEM((STEPS3, C3, 1), F32),
             pltpu.VMEM((KTOP, HID), F32),
@@ -766,6 +789,7 @@
             pltpu.VMEM((2, 16, LANES), F32),
             pltpu.VMEM((CHAN, 16, LANES), F32),
             pltpu.VMEM((ROWS, 1, LANES), F32),
+            pltpu.VMEM((8, LANES), F32),
             tuple(inner(KMID, WIDE, C2) for _ in range(2)),
             inner(KTOP, NTOP, C3),
             pltpu.SemaphoreType.DMA,

time: 34.1 us -> 33.7 us (0.988)
  Pallas kernels: 33.3 us -> 32.9 us
    pallas_call x1, Pallas kernels: 32.6 us -> 32.3 us  [body(): pl.pallas_call(kernel, out_shape=(pltpu.VMEM((8 * 12, COLS), F32), pltpu....]
where the time goes in v4:
time: 33.7 us; the launch traced here: 33.6 us
  Pallas kernels  32.9 us (98%)
  between operations  0.65 us (2%)
    pallas_call x1, Pallas kernels, body(): pl.pallas_call(kernel, out_shape=(pltpu.VMEM((8 * 12, COLS), F32), pltpu....  32.3 us

profile of v4, /device:TPU:1, one launch (start us, length us, event | category | flops | bytes accessed | tf_op | source)
XLA Modules:
  0.0 33.6 jit_solution(15775129921952318492)
XLA Ops:
  0.6 32.3 %shard_map.238 = (f32[96,32]{1,0:T(8,128)S(1)}, f32[1,4,16,48]{3,2,1,0:T(8,128)S(1)}, f32[1,128]{1,0:T(1,128)S(1)}) custom-call(f32[8,24,32]{2,1,0:T(8,128)} %bitcast.9, f32[3,24]{1,0:T(4,128)} %shift_mid.1, f32[3,24]{1,0:T(4,128)} %gain_mid.1, f32[3,24,24]{2,1,0:T(8,128)} %lower_mid.1, f32[3,24,24]{2,1,0:T(8,128)} %upper_mid.1, f32[3,24]{1,0:T(4,128)} %diag_mid.1, ...), custom_call_target="tpu_custom_call" | custom-call | tf_op jit(solution)/shard_map/pallas_call | solution.py:751
  32.9 0.7 %shard_map.239 = (f32[96,32]{1,0:T(8,128)}, f32[1,4,16,48]{3,2,1,0:T(8,128)}, f32[1,128]{1,0:T(1,128)}) custom-call(f32[96,32]{1,0:T(8,128)S(1)} %get-tuple-element.9.latent_mid, f32[1,4,16,48]{3,2,1,0:T(8,128)S(1)} %get-tuple-element.10.latent_top, f32[1,128]{1,0:T(1,128)S(1)} %get-tuple-element.11.loglik), custom_call_target="tpu_custom_call" | custom-call | tf_op jit(solution)/shard_map/pallas_call | solution.py:807

commit v5 on v4

--- a/solution.py
+++ b/solution.py
@@ -332,17 +332,13 @@
     ]
     for load in small_loads:
         load.start()
-    weight_loads = []
-    for s in range(STEPS2):
-        for src, dst in ((second_mid, second2), (first_mid, first2), (third_mid, third2)):
-            weight_loads.append(
-                pltpu.make_async_copy(src.at[s], dst.at[s], weight_sem.at[len(weight_loads)])
-            )
-    for s in range(STEPS3):
-        for src, dst in ((second_top, second3), (first_top, first3), (third_top, third3)):
-            weight_loads.append(
-                pltpu.make_async_copy(src.at[s], dst.at[s], weight_sem.at[len(weight_loads)])
-            )
+    given_weights = (second_mid, first_mid, third_mid, second_top, first_top, third_top)
+    kept_weights = (second2, first2, third2, second3, first3, third3)
+    weight_loads = [
+        pltpu.make_async_copy(src, dst, weight_sem.at[i])
+        for i, (src, dst) in enumerate(zip(given_weights, kept_weights))
+    ]
+
     def in_image(d, body):
         if d == 0:
             body()
@@ -416,8 +412,9 @@
         base[...] = jnp.where(corner, logdets, 0.0)
 
     def prepare_mid(s):
-        for i in range(3):
-            weight_loads[3 * s + i].wait()
+        if s == 0:
+            for load in weight_loads[:3]:
+                load.wait()
         w2_mid[s] = second2[s].T
         tall[...] = jnp.zeros_like(tall)
         for t in range(9):
@@ -429,8 +426,9 @@
             w3_mid[s, C2 * t : C2 * (t + 1), :] = dot(to_rows, third2[s, t]).astype(BF16)
 
     def prepare_top(s):
-        for i in range(3):
-            weight_loads[3 * STEPS2 + 3 * s + i].wait()
+        if s == 0:
+            for load in weight_loads[3:]:
+                load.wait()
         w2_top[s] = second3[s].T
         for t in range(9):
             tall[24 * t : 24 * (t + 1), :] = first3[s, t].astype(F32)
@@ -794,7 +792,7 @@
             inner(KTOP, NTOP, C3),
             pltpu.SemaphoreType.DMA,
             pltpu.SemaphoreType.DMA((16,)),
-            pltpu.SemaphoreType.DMA((15,)),
+            pltpu.SemaphoreType.DMA((6,)),
             pltpu.SemaphoreType.DMA,
             pltpu.SemaphoreType.DMA((BLOCKS,)),
             pltpu.SemaphoreType.DMA,

time: 33.7 us -> 33.6 us (level)
  no operation moved by 1% of the time
where the time goes in v5:
time: 33.6 us; the launch traced here: 33.5 us
  Pallas kernels  32.8 us (98%)
  between operations  0.65 us (2%)
    pallas_call x1, Pallas kernels, body(): pl.pallas_call(kernel, out_shape=(pltpu.VMEM((8 * 12, COLS), F32), pltpu....  32.2 us

profile of v5, /device:TPU:1, one launch (start us, length us, event | category | flops | bytes accessed | tf_op | source)
XLA Modules:
  0.0 33.5 jit_solution(2572387013354225949)
XLA Ops:
  0.6 32.2 %shard_map.238 = (f32[96,32]{1,0:T(8,128)S(1)}, f32[1,4,16,48]{3,2,1,0:T(8,128)S(1)}, f32[1,128]{1,0:T(1,128)S(1)}) custom-call(f32[8,24,32]{2,1,0:T(8,128)} %bitcast.9, f32[3,24]{1,0:T(4,128)} %shift_mid.1, f32[3,24]{1,0:T(4,128)} %gain_mid.1, f32[3,24,24]{2,1,0:T(8,128)} %lower_mid.1, f32[3,24,24]{2,1,0:T(8,128)} %upper_mid.1, f32[3,24]{1,0:T(4,128)} %diag_mid.1, ...), custom_call_target="tpu_custom_call" | custom-call | tf_op jit(solution)/shard_map/pallas_call | solution.py:749
  32.8 0.7 %shard_map.239 = (f32[96,32]{1,0:T(8,128)}, f32[1,4,16,48]{3,2,1,0:T(8,128)}, f32[1,128]{1,0:T(1,128)}) custom-call(f32[96,32]{1,0:T(8,128)S(1)} %get-tuple-element.9.latent_mid, f32[1,4,16,48]{3,2,1,0:T(8,128)S(1)} %get-tuple-element.10.latent_top, f32[1,128]{1,0:T(1,128)S(1)} %get-tuple-element.11.loglik), custom_call_target="tpu_custom_call" | custom-call | tf_op jit(solution)/shard_map/pallas_call | solution.py:805

commit v6 on v5

--- a/solution.py
+++ b/solution.py
@@ -462,6 +462,7 @@
         for k in range(3):
             part = mixed_in[8 * k : 8 * k + 8, LANES * (i // 4) : LANES * (i // 4 + 1)]
             tile = jnp.where(group == k, turned(part, COLS * (i % 4 - k)), tile)
+        tile = pltpu.roll(tile, COLS * (c % 4), 1)
         packed[i] = tile
         packed_half[i] = tile.astype(BF16)
 
@@ -542,9 +543,8 @@
             for j in range(4):
                 at = 4 * g + j
                 part = own_rows[at - 16] if 16 <= at < 24 else arrived[at].astype(F32)
-                part = turned(part, COLS * (k - j))
-                tile = part if tile is None else jnp.where(group == j, part, tile)
-            rows.append(tile)
+                tile = part if tile is None else jnp.where(group == (j + k) % 4, part, tile)
+            rows.append(turned(tile, COLS * k) if k else tile)
         return jnp.concatenate(rows, axis=0)
 
     steps = []

time: 33.6 us -> 33.6 us (level)
  no operation moved by 1% of the time
where the time goes in v6:
time: 33.6 us; the launch traced here: 33.5 us
  Pallas kernels  32.8 us (98%)
  between operations  0.65 us (2%)
    pallas_call x1, Pallas kernels, body(): pl.pallas_call(kernel, out_shape=(pltpu.VMEM((8 * 12, COLS), F32), pltpu....  32.2 us

profile of v6, /device:TPU:1, one launch (start us, length us, event | category | flops | bytes accessed | tf_op | source)
XLA Modules:
  0.0 33.5 jit_solution(17017674733209392944)
XLA Ops:
  0.6 32.2 %shard_map.238 = (f32[96,32]{1,0:T(8,128)S(1)}, f32[1,4,16,48]{3,2,1,0:T(8,128)S(1)}, f32[1,128]{1,0:T(1,128)S(1)}) custom-call(f32[8,24,32]{2,1,0:T(8,128)} %bitcast.9, f32[3,24]{1,0:T(4,128)} %shift_mid.1, f32[3,24]{1,0:T(4,128)} %gain_mid.1, f32[3,24,24]{2,1,0:T(8,128)} %lower_mid.1, f32[3,24,24]{2,1,0:T(8,128)} %upper_mid.1, f32[3,24]{1,0:T(4,128)} %diag_mid.1, ...), custom_call_target="tpu_custom_call" | custom-call | tf_op jit(solution)/shard_map/pallas_call | solution.py:749
  32.8 0.7 %shard_map.239 = (f32[96,32]{1,0:T(8,128)}, f32[1,4,16,48]{3,2,1,0:T(8,128)}, f32[1,128]{1,0:T(1,128)}) custom-call(f32[96,32]{1,0:T(8,128)S(1)} %get-tuple-element.9.latent_mid, f32[1,4,16,48]{3,2,1,0:T(8,128)S(1)} %get-tuple-element.10.latent_top, f32[1,128]{1,0:T(1,128)S(1)} %get-tuple-element.11.loglik), custom_call_target="tpu_custom_call" | custom-call | tf_op jit(solution)/shard_map/pallas_call | solution.py:805
